TPU v7x, 32 devices: a whole 2x2x4 slice. The times are simulated.
32 devices in a mesh: tok: 8 (over y, x, core), layer: 4 (over z).
Axes of the slice: x: 2, y: 2, z: 4, core: 2. Of those that a mesh axis runs over, the one named last changes fastest.
Arguments:
- activations: bfloat16 [4, 896, 5120], P(None, ('tok', 'layer')), may hold values from -9 to 9
- pos_weight: bfloat16 [4, 48, 5120], P('layer', None, 'tok'), may hold values from -1 to 1
- depth_weight: bfloat16 [4, 128, 5120], P('layer', None, 'tok'), may hold values from -0.01953125 to 0.01953125
- tags: int32 [896], P(('tok', 'layer')), may hold values from 0 to 47
- depths: int32 [896], P(('tok', 'layer')), may hold values from 2 to 14
- counts: int32 [32], P(('tok', 'layer')), may hold values from 1 to 28, 560 in all
Outputs:
- pos_grad: float32 [4, 48, 5120], P('layer', None, 'tok')
- depth_grad: float32 [4, 128, 5120], P('layer', None, 'tok')
Inputs may be any that keep to these rules, and one draw needn't show every extreme that they name: counts[d] is the number of live slots among device d's 28 slots, which are its first ones; the largest count equals 28.
All inputs are finite; a program needn't handle non-finite values.
Results may differ from a plain program's by a relative error of at most 0.0042.
Values may be sent and summed in bfloat16 or wider, within the bound.
No kernel may reach another device: no remote copies, remote signals or barrier semaphores. Data moves between devices by JAX's collectives and lax.ppermute only.
A program may use at most 64 MiB of HBM per device.

v0:
```python
import functools

import jax
import jax.numpy as jnp
from jax import lax
from jax.experimental import pallas as pl
from jax.experimental.pallas import tpu as pltpu
from jax.sharding import PartitionSpec as P


LANES = 128


def contract(left, right):
    return lax.dot_general(
        left, right, (((1,), (1,)), ((), ())), preferred_element_type=jnp.float32
    )


def steps(count):
    width = count.bit_length() - 2
    chips = sorted(range(1, count // 2), key=lambda c: (-c.bit_count(), c))
    mirrored = [sum((c >> n & 1) << (width - 1 - n) for n in range(width)) for c in chips]
    return [(0, 0)] + [(2 * a, 2 * b) for a, b in zip(chips, mirrored)]


def peer(tok, step):
    first, second = step
    if isinstance(tok, int):
        return tok ^ (second if tok % 2 else first)
    return tok ^ jnp.where(tok % 2 == 0, first, second)


def swap(value, step):
    pairs = [(i, peer(i, step)) for i in range(lax.axis_size("tok"))]
    return lax.ppermute(value, "tok", pairs)


def gray(i):
    return i ^ (i >> 1)


def ungray(i, count):
    total = i
    for n in range(1, count.bit_length()):
        total = total ^ (i >> n)
    return total


def ring_shifts(count):
    return [1, count - 1] + list(range(2, count - 1))


def ring_target(i, shift, count):
    return gray((ungray(i, count) + shift) % count)


def spans(slots, pieces):
    base = slots // 8 * 8
    return [(p, 0, base) for p in range(pieces)] + [
        (p, base, slots) for p in range(pieces) if base < slots
    ]


def tile_rows(slots, lo, hi, tile):
    base = slots // 8 * 8
    start = tile // 2 * 2 * slots
    if lo < base:
        start += tile % 2 * base
    else:
        start += 2 * base + tile % 2 * (slots - base)
    return slice(start, start + hi - lo)


def round_up(value, step):
    return -(-value // step) * step


def pick_rows(held, target, out, slots, layers, tiles):
    base = slots // 8 * 8
    for t in tiles:
        rows = held[t, pl.ds(target, slots, stride=layers), :].astype(out.dtype)
        out[tile_rows(slots, 0, base, t), :] = rows[:base]
        if base < slots:
            out[tile_rows(slots, base, slots, t), :] = rows[base:]


def first_kernel(me, act, pos, depth, out, held, probe, raw, act_sems, sems, *, slots, layers):
    width = act.shape[2]
    parts = act_sems.shape[0]
    step = width // parts
    tag_count = pos.shape[1]
    loads = [
        pltpu.make_async_copy(
            act.at[:, :, pl.ds(n * step, step)], raw.at[:, :, pl.ds(n * step, step)], act_sems.at[n]
        )
        for n in range(parts)
    ]
    others = [
        pltpu.make_async_copy(pos.at[0], probe.at[:tag_count], sems.at[0]),
        pltpu.make_async_copy(depth.at[0], probe.at[tag_count:], sems.at[1]),
    ]
    for copy in loads + others:
        copy.start()
    target = ring_target(me[0], ring_shifts(layers)[0], layers)
    for n in range(parts):
        loads[n].wait()
        tiles = range(n * step // LANES, (n + 1) * step // LANES)
        for t in tiles:
            for s in range(slots):
                held[t, s * layers : (s + 1) * layers, :] = raw[
                    s, :, t * LANES : (t + 1) * LANES
                ].astype(jnp.float32)
        pick_rows(held, target, out, slots, layers, tiles)
    for copy in others:
        copy.wait()


def rest_kernel(me, held, *outs, slots, layers):
    targets = [me[0]] + [ring_target(me[0], s, layers) for s in ring_shifts(layers)[1:]]
    for target, out in zip(targets, outs):
        pick_rows(held, target, out, slots, layers, range(held.shape[0]))


def share_kernel(me, rows, probe, *outs, peers):
    grads, cols = probe.shape
    piece = outs[0].shape[0] - cols // LANES * grads
    for step, out in zip(peers, outs):
        out[:piece, :] = rows[pl.ds(chip_start(me[0], step, piece), piece), :]
        for t in range(cols // LANES):
            out[piece + t * grads : piece + (t + 1) * grads, :] = probe[
                :, t * LANES : (t + 1) * LANES
            ]


def cut_kernel(me, *refs, pieces, peers):
    parts, outs = refs[:pieces], refs[pieces:]
    piece = outs[0].shape[0] // pieces
    for step, out in zip(peers, outs):
        start = chip_start(me[0], step, piece)
        for n, part in enumerate(parts):
            out[n * piece : (n + 1) * piece, :] = part[pl.ds(start, piece), :]


def chip_start(tok, step, piece):
    return pl.multiple_of((peer(tok, step) // 2) * piece, 8)


def score_kernel(me, *refs, pieces, blocks, send, slots, tags, rank, peers):
    parts = refs[:pieces]
    probes = refs[pieces : pieces + len(blocks)]
    tokens = refs[pieces + len(blocks) : 2 * pieces + len(blocks)]
    outs, rows = refs[2 * pieces + len(blocks) : -1], refs[-1]
    grads = tags + rank
    tiles = rows.shape[1] // LANES
    tok_tiles = tiles // len(blocks)
    cols = tok_tiles * LANES
    piece = 2 * tok_tiles * slots
    order = spans(slots, pieces)
    at, facts = 0, []
    for p, lo, hi in order:
        for t in range(tiles):
            rows[at : at + hi - lo, t * LANES : (t + 1) * LANES] = parts[p][
                tile_rows(slots, lo, hi, t), :
            ]
        facts.append(tokens[p][:, lo:hi])
        at += hi - lo
    fact = jnp.concatenate(facts, axis=1)
    scores = None
    for (step, flip), block in zip(blocks, probes):
        spot = pl.ds(pl.multiple_of(peer(me[0] ^ flip, step) * cols, LANES), cols)
        probe = jnp.concatenate(
            [block[piece + t * grads : piece + (t + 1) * grads, :] for t in range(tok_tiles)], axis=1
        )
        part = contract(probe, rows[:, spot])
        scores = part if scores is None else scores + part
    logits, hidden = scores[:tags], scores[tags:]
    tag_row, depth_row, count_row, place = fact[0:1], fact[1:2], fact[2:3], fact[3:4]
    scale = jnp.where(place < count_row, 1.0 / count_row.astype(jnp.float32), jnp.float32(0.0))
    top = jnp.max(logits, axis=0, keepdims=True)
    expo = jnp.exp(logits - top)
    probabilities = expo / jnp.sum(expo, axis=0, keepdims=True)
    tag_at = lax.broadcasted_iota(jnp.int32, logits.shape, 0)
    onehot = (tag_at == tag_row).astype(jnp.float32)
    g_pos = (probabilities - onehot) * scale
    predicted = jnp.sum(hidden * hidden, axis=0, keepdims=True)
    g_depth = hidden * ((predicted - depth_row.astype(jnp.float32)) * scale)
    joined = jnp.concatenate([g_pos, g_depth], axis=0)
    folds = LANES // joined.shape[1]
    height = outs[0].shape[0] - piece
    if height * folds > grads:
        filler = jnp.zeros((height * folds - grads, joined.shape[1]), jnp.float32)
        joined = jnp.concatenate([joined, filler], axis=0)
    joined = jnp.concatenate([joined[n * height : (n + 1) * height] for n in range(folds)], axis=1)
    if joined.shape[1] < LANES:
        filler = jnp.zeros((height, LANES - joined.shape[1]), jnp.float32)
        joined = jnp.concatenate([joined, filler], axis=1)
    joined = joined.astype(jnp.bfloat16)
    for step, out in zip(peers, outs):
        out[:piece, :] = parts[send][pl.ds(chip_start(me[0], step, piece), piece), :]
        out[piece:, :] = joined


def fold_height(grads, tokens):
    folds = LANES // tokens
    return grads if folds == 1 else round_up(-(-grads // folds), 16)


def grad_kernel(me, *refs, chips, slots, layers):
    sets = [refs[n * chips : (n + 1) * chips] for n in range(layers)]
    other, left, right = refs[layers * chips :]
    grads, cols = other.shape
    tiles = 2 * cols // LANES
    piece = tiles * slots
    first = (layers - 1) * slots
    second = round_up(first, 8)
    folds = LANES // slots
    for c in range(chips):
        head = sets[1][c][piece:, :].astype(jnp.float32)
        tail = sets[-1][c][piece:, :].astype(jnp.float32)
        tail = jnp.concatenate([tail[:, n * slots : (n + 1) * slots] for n in range(folds)], axis=0)
        both = [head[:, :second], tail[:grads]]
        if second + slots < LANES:
            both.append(jnp.zeros((grads, LANES - second - slots), jnp.float32))
        at = c * LANES
        left[:, at : at + LANES] = jnp.concatenate(both, axis=1).astype(left.dtype)
        gaps = []
        for start, members in ((0, range(layers - 1)), (second, range(layers - 1, layers))):
            at = c * LANES + start
            for p, lo, hi in spans(slots, len(members)):
                for t in range(tiles):
                    right[at : at + hi - lo, t * LANES : (t + 1) * LANES] = sets[members[p]][c][
                        tile_rows(slots, lo, hi, t), :
                    ]
                at += hi - lo
            gaps.append((at, c * LANES + (second if start == 0 else LANES)))
        for lo, hi in gaps:
            if lo < hi:
                right[lo:hi, :] = jnp.zeros((hi - lo, 2 * cols), right.dtype)
    other[...] = half_grad(left, right, 1 - me[0] % 2, cols).astype(other.dtype)


def half_grad(left, right, half, cols):
    spot = pl.ds(pl.multiple_of(half * cols, LANES), cols)
    return jnp.dot(left[...], right[:, spot], preferred_element_type=jnp.float32)


def mine_kernel(me, left, right, mine):
    mine[...] = half_grad(left, right, me[0] % 2, mine.shape[1])


def join_kernel(mine, other, pos_out, depth_out):
    tags = pos_out.shape[1]
    pos_out[0] = mine[:tags] + other[:tags].astype(jnp.float32)
    depth_out[0] = mine[tags:] + other[tags:].astype(jnp.float32)


def call(vmem, kernel, outs, scratch, scalars, *values, spaces=()):
    local = pl.BlockSpec(memory_space=pltpu.VMEM)
    specs = [pl.BlockSpec(memory_space=pltpu.SMEM)] * len(scalars)
    specs += [pl.BlockSpec(memory_space=s) for s in spaces]
    specs += [local] * (len(values) - len(spaces))
    return pl.pallas_call(
        kernel,
        out_shape=outs,
        in_specs=specs,
        out_specs=[local] * len(outs),
        scratch_shapes=scratch,
        compiler_params=pltpu.CompilerParams(vmem_limit_bytes=vmem << 20),
    )(*scalars, *values)


def fast(activations, pos_weight, depth_weight, tags, depths, counts):
    layer_count, tok_count = lax.axis_size("layer"), lax.axis_size("tok")
    tag_count, cols = pos_weight.shape[1:]
    rank = depth_weight.shape[1]
    slots = tags.shape[0]
    layers, _, width = activations.shape
    bf16, f32, i32 = jnp.bfloat16, jnp.float32, jnp.int32
    shape = jax.ShapeDtypeStruct
    grads = tag_count + rank
    layer_at = lax.axis_index("layer").astype(i32)[None]
    tok_at = lax.axis_index("tok").astype(i32)[None]
    peers = steps(tok_count)
    piece = 2 * cols // LANES * slots

    def exchange(values):
        return [values[0]] + [swap(v, step) for step, v in zip(peers[1:], values[1:])]

    message = shape((width // LANES * slots, LANES), bf16)
    held_shape = (width // LANES, slots * layers, LANES)
    shifts = ring_shifts(layer_count)

    def along(value, shift):
        pairs = [(i, ring_target(i, shift, layer_count)) for i in range(layer_count)]
        return lax.ppermute(value, "layer", pairs)

    head, held, probe = call(
        12, functools.partial(first_kernel, slots=slots, layers=layers),
        [message, shape(held_shape, f32), shape((grads, cols), bf16)],
        [
            pltpu.VMEM((slots, layers, width), bf16),
            pltpu.SemaphoreType.DMA((4,)),
            pltpu.SemaphoreType.DMA((2,)),
        ],
        [layer_at],
        *[
            pltpu.with_memory_space_constraint(v, pltpu.HBM)
            for v in (jnp.transpose(activations, (1, 0, 2)), pos_weight, depth_weight)
        ],
        spaces=[pltpu.HBM] * 3,
    )
    own, *others = call(
        4, functools.partial(rest_kernel, slots=slots, layers=layers),
        [message] * (layers - 1), [], [layer_at], held,
    )
    pieces = [own] + [along(v, shift) for v, shift in zip([head] + others, shifts)]
    fact = jnp.stack([tags, depths, jnp.broadcast_to(counts, tags.shape), jnp.arange(slots, dtype=i32)])
    facts = [fact] + [along(fact, shift) for shift in shifts]
    shares = call(
        4, functools.partial(share_kernel, peers=peers),
        [shape((piece + cols // LANES * grads, LANES), bf16)] * len(peers),
        [], [tok_at], own, probe,
    )
    shares = exchange(shares)
    probes = shares + [swap(v, (1, 1)) for v in shares]
    blocks = [(step, 0) for step in peers] + [(step, 1) for step in peers]
    early = [
        exchange(
            call(
                4, functools.partial(cut_kernel, pieces=1, peers=peers),
                [shape((piece, LANES), bf16)] * len(peers), [], [tok_at], pieces[n],
            ),
        )
        for n in range(2, layers - 1)
    ]

    def score(members, send):
        outs = call(
            12,
            functools.partial(
                score_kernel, pieces=len(members), blocks=blocks, send=send, slots=slots,
                tags=tag_count, rank=rank, peers=peers,
            ),
            [shape((piece + fold_height(grads, len(members) * slots), LANES), bf16)] * len(peers),
            [pltpu.VMEM((len(members) * slots, width), bf16)],
            [tok_at], *[pieces[n] for n in members], *probes, *[facts[n] for n in members],
        )
        return exchange(outs)

    middle = score(range(layers - 1), 1)
    late = score([layers - 1], 0)
    other, left, right = call(
        8,
        functools.partial(grad_kernel, chips=len(peers), slots=slots, layers=layer_count),
        [
            shape((grads, cols), bf16),
            shape((grads, len(peers) * LANES), bf16),
            shape((len(peers) * LANES, 2 * cols), bf16),
        ],
        [], [tok_at], *shares, *middle, *[v for part in early for v in part], *late,
    )
    other = swap(other, (1, 1))
    (mine,) = call(4, mine_kernel, [shape((grads, cols), f32)], [], [tok_at], left, right)
    return call(
        4, join_kernel,
        [shape((1, tag_count, cols), f32), shape((1, rank, cols), f32)], [], [], mine, other,
    )


def general(activations, pos_weight, depth_weight, tags, depths, counts):
    tag_count = pos_weight.shape[1]
    slots = tags.shape[0]
    rows = lax.all_to_all(activations, "layer", split_axis=0, concat_axis=1, tiled=True)[0]
    probe = jnp.concatenate([pos_weight[0], depth_weight[0]], axis=0)
    probe = lax.all_gather(probe, "tok", axis=1, tiled=True)
    scores = contract(rows, probe)
    logits, hidden = scores[:, :tag_count], scores[:, tag_count:]
    facts = jnp.stack([tags, depths, jnp.broadcast_to(counts, tags.shape)])
    tag_row, depth_row, block_count = lax.all_gather(facts, "layer", axis=1, tiled=True)
    live = jnp.arange(rows.shape[0], dtype=jnp.int32) % slots < block_count
    scale = jnp.where(live, 1.0 / block_count.astype(jnp.float32), jnp.float32(0.0))
    expo = jnp.exp(logits - jnp.max(logits, axis=1, keepdims=True))
    probabilities = expo / jnp.sum(expo, axis=1, keepdims=True)
    onehot = (tag_row[:, None] == jnp.arange(tag_count, dtype=jnp.int32)[None, :]).astype(jnp.float32)
    g_pos = (probabilities - onehot) * scale[:, None]
    predicted = jnp.sum(hidden * hidden, axis=1)
    g_depth = hidden * ((predicted - depth_row.astype(jnp.float32)) * scale)[:, None]
    joined = jnp.concatenate([g_pos, g_depth], axis=1).astype(jnp.bfloat16)
    share = lax.dot_general(
        joined, rows, (((0,), (0,)), ((), ())), preferred_element_type=jnp.float32
    )
    summed = lax.psum_scatter(share, "tok", scatter_dimension=1, tiled=True)
    return summed[None, :tag_count], summed[None, tag_count:]


def fits(layer_count, tok_count, activations, pos_weight, depth_weight):
    layers, slots, width = activations.shape
    cols = pos_weight.shape[2]
    grads = pos_weight.shape[1] + depth_weight.shape[1]
    return (
        layers == layer_count
        and layers >= 4
        and layers & (layers - 1) == 0
        and tok_count >= 4
        and tok_count & (tok_count - 1) == 0
        and cols % LANES == 0
        and width == cols * tok_count
        and slots % 4 == 0
        and slots >= 8
        and round_up((layers - 1) * slots, 8) + slots <= LANES
        and grads % 16 == 0
        and pos_weight.shape[1] % 16 == 0
    )


def local(activations, pos_weight, depth_weight, tags, depths, counts):
    sizes = lax.axis_size("layer"), lax.axis_size("tok")
    if fits(*sizes, activations, pos_weight, depth_weight):
        return fast(activations, pos_weight, depth_weight, tags, depths, counts)
    return general(activations, pos_weight, depth_weight, tags, depths, counts)


def solution(mesh):
    in_specs = (
        P(None, ("tok", "layer"), None),
        P("layer", None, "tok"),
        P("layer", None, "tok"),
        P(("tok", "layer")),
        P(("tok", "layer")),
        P(("tok", "layer")),
    )
    out_specs = (P("layer", None, "tok"), P("layer", None, "tok"))

    return jax.shard_map(local, mesh=mesh, in_specs=in_specs, out_specs=out_specs, check_vma=False)
```

profile of v0, /device:TPU:0, one launch (start us, length us, event | category | flops | bytes accessed | tf_op | source)
XLA Modules:
  0.0 57.7 jit_solution(10568838213185859941)
XLA Ops:
  0.6 1.4 %shard_map.80 = (bf16[1120,128]{1,0:T(8,128)(2,1)S(1)}, f32[40,112,128]{2,1,0:T(8,128)S(1)}, bf16[176,640]{1,0:T(8,128)(2,1)S(1)}) custom-call(s32[1]{0:T(128)} %bitcast.1.me, bf16[28,4,5120]{2,1,0:T(4,128)(2,1)} %bitcast.6, bf16[1,48,640]{2,1,0:T(8,128)(2,1)} %pos.1, bf16[1,128,640]{2,1,0:T(8,128)(2,1)} %depth.1), custom_call_target="tpu_custom_call" | custom-call | tf_op jit(solution)/shard_map/pallas_call | solution.py:263
  2.0 0.0 copy-start
  2.0 0.0 copy-start.1
  2.1 0.2 shard_map.81
  2.3 0.1 shard_map.82
  2.4 4.0 %collective-permute-start = (bf16[1160,128]{1,0:T(8,128)(2,1)S(1)}, bf16[1160,128]{1,0:T(8,128)(2,1)S(1)}, u32[]{:S(2)}, u32[]{:S(2)}) collective-permute-start(bf16[1160,128]{1,0:T(8,128)(2,1)S(1)} %get-tuple-element.31), channel_id=1, source_target_pairs={{0,24},{4,28},{8,16},{12,20},{16,8},{20,12},{24,0},{28,4},{1,25},{... | collective-permute-start | bytes 890888 | tf_op jit(solution)/shard_map/ppermute | solution.py:36
  6.4 0.5 collective-permute-start.1
  7.0 0.1 collective-permute-start.2
  7.1 3.0 %collective-permute-start.4 = (bf16[1120,128]{1,0:T(8,128)(2,1)S(1)}, bf16[1120,128]{1,0:T(8,128)(2,1)S(1)}, u32[]{:S(2)}, u32[]{:S(2)}) collective-permute-start(bf16[1120,128]{1,0:T(8,128)(2,1)S(1)} %get-tuple-element.35), channel_id=1, source_target_pairs={{0,2},{1,0},{2,3},{3,1},{4,6},{5,4},{6,7},{7,5},{8,10},{9,8},{10,1... | collective-permute-start | bytes 860168 | tf_op jit(solution)/shard_map/ppermute | solution.py:296
  10.7 0.1 pad.2.clone
  10.8 0.1 pad_add_fusion.refs_11_
  10.9 1.4 %collective-permute-start.18 = (s32[4,28]{1,0:T(4,128)S(1)}, s32[4,28]{1,0:T(4,128)S(1)}, u32[]{:S(2)}, u32[]{:S(2)}) collective-permute-start(s32[4,28]{1,0:T(4,128)S(1)} %pad_add_fusion.refs_11_), channel_id=1, source_target_pairs={{0,3},{1,2},{2,1},{3,0},{4,7},{5,6},{6,5},{7,4},{8,11},{9,10},{10,... | collective-permute-start | bytes 1352 | tf_op jit(solution)/shard_map/ppermute | solution.py:296
  12.2 5.0 %collective-permute-done.18.refs_9_ = s32[4,28]{1,0:T(4,128)S(1)} collective-permute-done((s32[4,28]{1,0:T(4,128)S(1)}, s32[4,28]{1,0:T(4,128)S(1)}, u32[]{:S(2)}, u32[]{:S(2)}) %collective-permute-start.18) | collective-permute-done | bytes 480 | tf_op jit(solution)/shard_map/ppermute | solution.py:296
  17.3 2.5 %collective-permute-start.17 = (bf16[1120,128]{1,0:T(8,128)(2,1)S(1)}, bf16[1120,128]{1,0:T(8,128)(2,1)S(1)}, u32[]{:S(2)}, u32[]{:S(2)}) collective-permute-start(bf16[1120,128]{1,0:T(8,128)(2,1)S(1)} %get-tuple-element.44), channel_id=1, source_target_pairs={{0,3},{1,2},{2,1},{3,0},{4,7},{5,6},{6,5},{7,4},{8,11},{9,10},{10,... | collective-permute-start | bytes 860168 | tf_op jit(solution)/shard_map/ppermute | solution.py:296
  19.7 0.0 collective-permute-done.4.refs_2_.refs_0_
  19.7 0.0 collective-permute-start.5
  19.7 0.0 collective-permute-done.refs_4_.refs_2_.refs_1_
  19.7 0.5 collective-permute-start.6
  20.3 0.0 collective-permute-done.1.refs_5_.refs_3_.refs_2_
  20.3 0.1 collective-permute-start.7
  20.3 0.4 collective-permute-start.8
  20.8 4.9 %collective-permute-done.17.refs_0_ = bf16[1120,128]{1,0:T(8,128)(2,1)S(1)} collective-permute-done((bf16[1120,128]{1,0:T(8,128)(2,1)S(1)}, bf16[1120,128]{1,0:T(8,128)(2,1)S(1)}, u32[]{:S(2)}, u32[]{:S(2)}) %collective-permute-start.17) | collective-permute-done | bytes 286752 | tf_op jit(solution)/shard_map/ppermute | solution.py:296
  25.7 4.3 %collective-permute-start.3 = (bf16[1120,128]{1,0:T(8,128)(2,1)S(1)}, bf16[1120,128]{1,0:T(8,128)(2,1)S(1)}, u32[]{:S(2)}, u32[]{:S(2)}) collective-permute-start(bf16[1120,128]{1,0:T(8,128)(2,1)S(1)} %get-tuple-element.34), channel_id=1, source_target_pairs={{0,1},{1,3},{2,0},{3,2},{4,5},{5,7},{6,4},{7,6},{8,9},{9,11},{10,8... | collective-permute-start | bytes 860168 | tf_op jit(solution)/shard_map/ppermute | solution.py:296
  30.1 2.5 %collective-permute-start.14 = (bf16[280,128]{1,0:T(8,128)(2,1)S(1)}, bf16[280,128]{1,0:T(8,128)(2,1)S(1)}, u32[]{:S(2)}, u32[]{:S(2)}) collective-permute-start(bf16[280,128]{1,0:T(8,128)(2,1)S(1)} %get-tuple-element.41), channel_id=1, source_target_pairs={{0,24},{4,28},{8,16},{12,20},{16,8},{20,12},{24,0},{28,4},{1,25},{... | collective-permute-start | bytes 215048 | tf_op jit(solution)/shard_map/ppermute | solution.py:36
  32.6 0.0 collective-permute-done.6.refs_8_.refs_6_
  32.6 0.5 collective-permute-start.15
  33.2 0.0 collective-permute-done.7.refs_9_.refs_7_
  33.2 0.0 collective-permute-done.8.refs_10_.refs_8_
  33.2 0.9 %shard_map.85 = (bf16[328,128]{1,0:T(8,128)(2,1)S(1)}, bf16[328,128]{1,0:T(8,128)(2,1)S(1)}, bf16[328,128]{1,0:T(8,128)(2,1)S(1)}, bf16[328,128]{1,0:T(8,128)(2,1)S(1)}) custom-call(s32[1]{0:T(128)} %bitcast.me, bf16[1120,128]{1,0:T(8,128)(2,1)S(1)} %collective-permute-done.17.refs_0_, bf16[1160,128]{1,0:T(8,128)(2,1)S(1)} %get-tuple-element.30.refs_3_.refs_1_.refs_0_, ...), custom_call_target="tpu_custom_call" | custom-call | tf_op jit(solution)/shard_map/pallas_call | solution.py:263
  34.0 1.5 %collective-permute-start.19 = (bf16[328,128]{1,0:T(8,128)(2,1)S(1)}, bf16[328,128]{1,0:T(8,128)(2,1)S(1)}, u32[]{:S(2)}, u32[]{:S(2)}) collective-permute-start(bf16[328,128]{1,0:T(8,128)(2,1)S(1)} %get-tuple-element.46), channel_id=1, source_target_pairs={{0,24},{4,28},{8,16},{12,20},{16,8},{20,12},{24,0},{28,4},{1,25},{... | collective-permute-start | bytes 251912 | tf_op jit(solution)/shard_map/ppermute | solution.py:36
  35.5 0.0 collective-permute-start.9
  35.5 4.5 %collective-permute-done.9.refs_12_ = s32[4,28]{1,0:T(4,128)S(1)} collective-permute-done((s32[4,28]{1,0:T(4,128)S(1)}, s32[4,28]{1,0:T(4,128)S(1)}, u32[]{:S(2)}, u32[]{:S(2)}) %collective-permute-start.9) | collective-permute-done | bytes 480 | tf_op jit(solution)/shard_map/ppermute | solution.py:296
  40.0 0.1 collective-permute-start.10
  40.1 3.5 %collective-permute-done.10.refs_13_ = s32[4,28]{1,0:T(4,128)S(1)} collective-permute-done((s32[4,28]{1,0:T(4,128)S(1)}, s32[4,28]{1,0:T(4,128)S(1)}, u32[]{:S(2)}, u32[]{:S(2)}) %collective-permute-start.10) | collective-permute-done | bytes 480 | tf_op jit(solution)/shard_map/ppermute | solution.py:296
  43.6 1.5 %collective-permute-start.16 = (bf16[280,128]{1,0:T(8,128)(2,1)S(1)}, bf16[280,128]{1,0:T(8,128)(2,1)S(1)}, u32[]{:S(2)}, u32[]{:S(2)}) collective-permute-start(bf16[280,128]{1,0:T(8,128)(2,1)S(1)} %get-tuple-element.43), channel_id=1, source_target_pairs={{0,16},{4,12},{8,24},{12,4},{16,0},{20,28},{24,8},{28,20},{1,17},{... | collective-permute-start | bytes 215048 | tf_op jit(solution)/shard_map/ppermute | solution.py:36
  45.1 0.9 %shard_map.83 = (bf16[456,128]{1,0:T(8,128)(2,1)S(1)}, bf16[456,128]{1,0:T(8,128)(2,1)S(1)}, bf16[456,128]{1,0:T(8,128)(2,1)S(1)}, bf16[456,128]{1,0:T(8,128)(2,1)S(1)}) custom-call(s32[1]{0:T(128)} %bitcast.me, bf16[1120,128]{1,0:T(8,128)(2,1)S(1)} %get-tuple-element.28.rows.refs_0_, bf16[1120,128]{1,0:T(8,128)(2,1)S(1)} %collective-permute-done.3.refs_1_, ...), custom_call_target="tpu_custom_call" | custom-call | tf_op jit(solution)/shard_map/pallas_call | solution.py:263
  46.1 0.5 collective-permute-start.11
  46.6 1.5 %collective-permute-start.12 = (bf16[456,128]{1,0:T(8,128)(2,1)S(1)}, bf16[456,128]{1,0:T(8,128)(2,1)S(1)}, u32[]{:S(2)}, u32[]{:S(2)}) collective-permute-start(bf16[456,128]{1,0:T(8,128)(2,1)S(1)} %get-tuple-element.38), channel_id=1, source_target_pairs={{0,8},{4,20},{8,0},{12,28},{16,24},{20,4},{24,16},{28,12},{1,9},{5... | collective-permute-start | bytes 350216 | tf_op jit(solution)/shard_map/ppermute | solution.py:36
  48.1 1.5 %collective-permute-start.13 = (bf16[456,128]{1,0:T(8,128)(2,1)S(1)}, bf16[456,128]{1,0:T(8,128)(2,1)S(1)}, u32[]{:S(2)}, u32[]{:S(2)}) collective-permute-start(bf16[456,128]{1,0:T(8,128)(2,1)S(1)} %get-tuple-element.39), channel_id=1, source_target_pairs={{0,16},{4,12},{8,24},{12,4},{16,0},{20,28},{24,8},{28,20},{1,17},{... | collective-permute-start | bytes 350216 | tf_op jit(solution)/shard_map/ppermute | solution.py:36
  49.6 0.5 collective-permute-start.20
  50.2 0.6 %collective-permute-start.21 = (bf16[328,128]{1,0:T(8,128)(2,1)S(1)}, bf16[328,128]{1,0:T(8,128)(2,1)S(1)}, u32[]{:S(2)}, u32[]{:S(2)}) collective-permute-start(bf16[328,128]{1,0:T(8,128)(2,1)S(1)} %get-tuple-element.48), channel_id=1, source_target_pairs={{0,16},{4,12},{8,24},{12,4},{16,0},{20,28},{24,8},{28,20},{1,17},{... | collective-permute-start | bytes 251912 | tf_op jit(solution)/shard_map/ppermute | solution.py:36
  50.8 3.3 %collective-permute-done.20.refs_14_ = bf16[328,128]{1,0:T(8,128)(2,1)S(1)} collective-permute-done((bf16[328,128]{1,0:T(8,128)(2,1)S(1)}, bf16[328,128]{1,0:T(8,128)(2,1)S(1)}, u32[]{:S(2)}, u32[]{:S(2)}) %collective-permute-start.20) | collective-permute-done | bytes 84000 | tf_op jit(solution)/shard_map/ppermute | solution.py:36
  54.1 0.5 collective-permute-done.21.refs_15_
  54.6 0.7 %shard_map.86 = (bf16[176,640]{1,0:T(8,128)(2,1)S(1)}, bf16[176,512]{1,0:T(8,128)(2,1)S(1)}, bf16[512,1280]{1,0:T(8,128)(2,1)S(1)}) custom-call(s32[1]{0:T(128)} %bitcast.me, bf16[1160,128]{1,0:T(8,128)(2,1)S(1)} %get-tuple-element.30.refs_3_.refs_1_.refs_0_, bf16[1160,128]{1,0:T(8,128)(2,1)S(1)} %collective-permute-done.refs_4_.refs_2_.refs_1_, ...), custom_call_target="tpu_custom_call" | custom-call | tf_op jit(solution)/shard_map/pallas_call | solution.py:263
  55.3 0.1 collective-permute-start.22
  55.4 0.3 shard_map.87.mine
  55.7 1.1 %collective-permute-done.22.other = bf16[176,640]{1,0:T(8,128)(2,1)S(1)} collective-permute-done((bf16[176,640]{1,0:T(8,128)(2,1)S(1)}, bf16[176,640]{1,0:T(8,128)(2,1)S(1)}, u32[]{:S(2)}, u32[]{:S(2)}) %collective-permute-start.22) | collective-permute-done | bytes 225312 | tf_op jit(solution)/shard_map/ppermute | solution.py:36
  56.9 0.8 %shard_map.88 = (f32[1,48,640]{2,1,0:T(8,128)}, f32[1,128,640]{2,1,0:T(8,128)}) custom-call(f32[176,640]{1,0:T(8,128)S(1)} %shard_map.87.mine, bf16[176,640]{1,0:T(8,128)(2,1)S(1)} %collective-permute-done.22.other), custom_call_target="tpu_custom_call" | custom-call | tf_op jit(solution)/shard_map/pallas_call | solution.py:263
  (14 shorter events, 0.1 us)
Async XLA Ops:
  2.0 8.8 %copy-start = (s32[28]{0:T(128)S(1)}, s32[28]{0:T(128)}, u32[]{:S(2)}) copy-start(s32[28]{0:T(128)} %param.10) | copy-start | bytes 340
  2.0 8.8 %copy-start.1 = (s32[28]{0:T(128)S(1)}, s32[28]{0:T(128)}, u32[]{:S(2)}) copy-start(s32[28]{0:T(128)} %param.9) | copy-start | bytes 340
  2.4 17.3 %collective-permute-start = (bf16[1160,128]{1,0:T(8,128)(2,1)S(1)}, bf16[1160,128]{1,0:T(8,128)(2,1)S(1)}, u32[]{:S(2)}, u32[]{:S(2)}) collective-permute-start(bf16[1160,128]{1,0:T(8,128)(2,1)S(1)} %get-tuple-element.31), channel_id=1, source_target_pairs={{0,24},{4,28},{8,16},{12,20},{16,8},{20,12},{24,0},{28,4},{1,25},{... | collective-permute-start | bytes 890888 | tf_op jit(solution)/shard_map/ppermute | solution.py:36
  6.4 13.8 %collective-permute-start.1 = (bf16[1160,128]{1,0:T(8,128)(2,1)S(1)}, bf16[1160,128]{1,0:T(8,128)(2,1)S(1)}, u32[]{:S(2)}, u32[]{:S(2)}) collective-permute-start(bf16[1160,128]{1,0:T(8,128)(2,1)S(1)} %get-tuple-element.32), channel_id=1, source_target_pairs={{0,8},{4,20},{8,0},{12,28},{16,24},{20,4},{24,16},{28,12},{1,9},{5... | collective-permute-start | bytes 890888 | tf_op jit(solution)/shard_map/ppermute | solution.py:36
  7.0 13.4 %collective-permute-start.2 = (bf16[1160,128]{1,0:T(8,128)(2,1)S(1)}, bf16[1160,128]{1,0:T(8,128)(2,1)S(1)}, u32[]{:S(2)}, u32[]{:S(2)}) collective-permute-start(bf16[1160,128]{1,0:T(8,128)(2,1)S(1)} %get-tuple-element.33), channel_id=1, source_target_pairs={{0,16},{4,12},{8,24},{12,4},{16,0},{20,28},{24,8},{28,20},{1,17},{... | collective-permute-start | bytes 890888 | tf_op jit(solution)/shard_map/ppermute | solution.py:36
  7.1 12.7 %collective-permute-start.4 = (bf16[1120,128]{1,0:T(8,128)(2,1)S(1)}, bf16[1120,128]{1,0:T(8,128)(2,1)S(1)}, u32[]{:S(2)}, u32[]{:S(2)}) collective-permute-start(bf16[1120,128]{1,0:T(8,128)(2,1)S(1)} %get-tuple-element.35), channel_id=1, source_target_pairs={{0,2},{1,0},{2,3},{3,1},{4,6},{5,4},{6,7},{7,5},{8,10},{9,8},{10,1... | collective-permute-start | bytes 860168 | tf_op jit(solution)/shard_map/ppermute | solution.py:296
  10.9 6.4 %collective-permute-start.18 = (s32[4,28]{1,0:T(4,128)S(1)}, s32[4,28]{1,0:T(4,128)S(1)}, u32[]{:S(2)}, u32[]{:S(2)}) collective-permute-start(s32[4,28]{1,0:T(4,128)S(1)} %pad_add_fusion.refs_11_), channel_id=1, source_target_pairs={{0,3},{1,2},{2,1},{3,0},{4,7},{5,6},{6,5},{7,4},{8,11},{9,10},{10,... | collective-permute-start | bytes 1352 | tf_op jit(solution)/shard_map/ppermute | solution.py:296
  17.3 8.5 %collective-permute-start.17 = (bf16[1120,128]{1,0:T(8,128)(2,1)S(1)}, bf16[1120,128]{1,0:T(8,128)(2,1)S(1)}, u32[]{:S(2)}, u32[]{:S(2)}) collective-permute-start(bf16[1120,128]{1,0:T(8,128)(2,1)S(1)} %get-tuple-element.44), channel_id=1, source_target_pairs={{0,3},{1,2},{2,1},{3,0},{4,7},{5,6},{6,5},{7,4},{8,11},{9,10},{10,... | collective-permute-start | bytes 860168 | tf_op jit(solution)/shard_map/ppermute | solution.py:296
  19.7 10.4 %collective-permute-start.5 = (bf16[1160,128]{1,0:T(8,128)(2,1)S(1)}, bf16[1160,128]{1,0:T(8,128)(2,1)S(1)}, u32[]{:S(2)}, u32[]{:S(2)}) collective-permute-start(bf16[1160,128]{1,0:T(8,128)(2,1)S(1)} %get-tuple-element.30.refs_3_.refs_1_.refs_0_), channel_id=1, source_target_pairs={{0,4},{4,0},{8,12},{12,8},{16,20},{20,16},{24,28},{28,24},{1,5},{5... | collective-permute-start | bytes 890888 | tf_op jit(solution)/shard_map/ppermute | solution.py:36
  19.7 12.9 %collective-permute-start.6 = (bf16[1160,128]{1,0:T(8,128)(2,1)S(1)}, bf16[1160,128]{1,0:T(8,128)(2,1)S(1)}, u32[]{:S(2)}, u32[]{:S(2)}) collective-permute-start(bf16[1160,128]{1,0:T(8,128)(2,1)S(1)} %collective-permute-done.refs_4_.refs_2_.refs_1_), channel_id=1, source_target_pairs={{0,4},{4,0},{8,12},{12,8},{16,20},{20,16},{24,28},{28,24},{1,5},{5... | collective-permute-start | bytes 890888 | tf_op jit(solution)/shard_map/ppermute | solution.py:36
  20.3 12.9 %collective-permute-start.7 = (bf16[1160,128]{1,0:T(8,128)(2,1)S(1)}, bf16[1160,128]{1,0:T(8,128)(2,1)S(1)}, u32[]{:S(2)}, u32[]{:S(2)}) collective-permute-start(bf16[1160,128]{1,0:T(8,128)(2,1)S(1)} %collective-permute-done.1.refs_5_.refs_3_.refs_2_), channel_id=1, source_target_pairs={{0,4},{4,0},{8,12},{12,8},{16,20},{20,16},{24,28},{28,24},{1,5},{5... | collective-permute-start | bytes 890888 | tf_op jit(solution)/shard_map/ppermute | solution.py:36
  20.3 12.8 %collective-permute-start.8 = (bf16[1160,128]{1,0:T(8,128)(2,1)S(1)}, bf16[1160,128]{1,0:T(8,128)(2,1)S(1)}, u32[]{:S(2)}, u32[]{:S(2)}) collective-permute-start(bf16[1160,128]{1,0:T(8,128)(2,1)S(1)} %collective-permute-done.2.refs_6_.refs_4_.refs_3_), channel_id=1, source_target_pairs={{0,4},{4,0},{8,12},{12,8},{16,20},{20,16},{24,28},{28,24},{1,5},{5... | collective-permute-start | bytes 890888 | tf_op jit(solution)/shard_map/ppermute | solution.py:36
  25.7 19.4 %collective-permute-start.3 = (bf16[1120,128]{1,0:T(8,128)(2,1)S(1)}, bf16[1120,128]{1,0:T(8,128)(2,1)S(1)}, u32[]{:S(2)}, u32[]{:S(2)}) collective-permute-start(bf16[1120,128]{1,0:T(8,128)(2,1)S(1)} %get-tuple-element.34), channel_id=1, source_target_pairs={{0,1},{1,3},{2,0},{3,2},{4,5},{5,7},{6,4},{7,6},{8,9},{9,11},{10,8... | collective-permute-start | bytes 860168 | tf_op jit(solution)/shard_map/ppermute | solution.py:296
  30.1 16.5 %collective-permute-start.14 = (bf16[280,128]{1,0:T(8,128)(2,1)S(1)}, bf16[280,128]{1,0:T(8,128)(2,1)S(1)}, u32[]{:S(2)}, u32[]{:S(2)}) collective-permute-start(bf16[280,128]{1,0:T(8,128)(2,1)S(1)} %get-tuple-element.41), channel_id=1, source_target_pairs={{0,24},{4,28},{8,16},{12,20},{16,8},{20,12},{24,0},{28,4},{1,25},{... | collective-permute-start | bytes 215048 | tf_op jit(solution)/shard_map/ppermute | solution.py:36
  32.6 15.5 %collective-permute-start.15 = (bf16[280,128]{1,0:T(8,128)(2,1)S(1)}, bf16[280,128]{1,0:T(8,128)(2,1)S(1)}, u32[]{:S(2)}, u32[]{:S(2)}) collective-permute-start(bf16[280,128]{1,0:T(8,128)(2,1)S(1)} %get-tuple-element.42), channel_id=1, source_target_pairs={{0,8},{4,20},{8,0},{12,28},{16,24},{20,4},{24,16},{28,12},{1,9},{5... | collective-permute-start | bytes 215048 | tf_op jit(solution)/shard_map/ppermute | solution.py:36
  34.0 16.1 %collective-permute-start.19 = (bf16[328,128]{1,0:T(8,128)(2,1)S(1)}, bf16[328,128]{1,0:T(8,128)(2,1)S(1)}, u32[]{:S(2)}, u32[]{:S(2)}) collective-permute-start(bf16[328,128]{1,0:T(8,128)(2,1)S(1)} %get-tuple-element.46), channel_id=1, source_target_pairs={{0,24},{4,28},{8,16},{12,20},{16,8},{20,12},{24,0},{28,4},{1,25},{... | collective-permute-start | bytes 251912 | tf_op jit(solution)/shard_map/ppermute | solution.py:36
  35.5 4.5 %collective-permute-start.9 = (s32[4,28]{1,0:T(4,128)S(1)}, s32[4,28]{1,0:T(4,128)S(1)}, u32[]{:S(2)}, u32[]{:S(2)}) collective-permute-start(s32[4,28]{1,0:T(4,128)S(1)} %pad_add_fusion.refs_11_), channel_id=1, source_target_pairs={{0,1},{1,3},{2,0},{3,2},{4,5},{5,7},{6,4},{7,6},{8,9},{9,11},{10,8... | collective-permute-start | bytes 1352 | tf_op jit(solution)/shard_map/ppermute | solution.py:296
  40.0 3.6 %collective-permute-start.10 = (s32[4,28]{1,0:T(4,128)S(1)}, s32[4,28]{1,0:T(4,128)S(1)}, u32[]{:S(2)}, u32[]{:S(2)}) collective-permute-start(s32[4,28]{1,0:T(4,128)S(1)} %pad_add_fusion.refs_11_), channel_id=1, source_target_pairs={{0,2},{1,0},{2,3},{3,1},{4,6},{5,4},{6,7},{7,5},{8,10},{9,8},{10,1... | collective-permute-start | bytes 1352 | tf_op jit(solution)/shard_map/ppermute | solution.py:296
  43.6 6.0 %collective-permute-start.16 = (bf16[280,128]{1,0:T(8,128)(2,1)S(1)}, bf16[280,128]{1,0:T(8,128)(2,1)S(1)}, u32[]{:S(2)}, u32[]{:S(2)}) collective-permute-start(bf16[280,128]{1,0:T(8,128)(2,1)S(1)} %get-tuple-element.43), channel_id=1, source_target_pairs={{0,16},{4,12},{8,24},{12,4},{16,0},{20,28},{24,8},{28,20},{1,17},{... | collective-permute-start | bytes 215048 | tf_op jit(solution)/shard_map/ppermute | solution.py:36
  46.1 8.6 %collective-permute-start.11 = (bf16[456,128]{1,0:T(8,128)(2,1)S(1)}, bf16[456,128]{1,0:T(8,128)(2,1)S(1)}, u32[]{:S(2)}, u32[]{:S(2)}) collective-permute-start(bf16[456,128]{1,0:T(8,128)(2,1)S(1)} %get-tuple-element.37), channel_id=1, source_target_pairs={{0,24},{4,28},{8,16},{12,20},{16,8},{20,12},{24,0},{28,4},{1,25},{... | collective-permute-start | bytes 350216 | tf_op jit(solution)/shard_map/ppermute | solution.py:36
  46.6 8.0 %collective-permute-start.12 = (bf16[456,128]{1,0:T(8,128)(2,1)S(1)}, bf16[456,128]{1,0:T(8,128)(2,1)S(1)}, u32[]{:S(2)}, u32[]{:S(2)}) collective-permute-start(bf16[456,128]{1,0:T(8,128)(2,1)S(1)} %get-tuple-element.38), channel_id=1, source_target_pairs={{0,8},{4,20},{8,0},{12,28},{16,24},{20,4},{24,16},{28,12},{1,9},{5... | collective-permute-start | bytes 350216 | tf_op jit(solution)/shard_map/ppermute | solution.py:36
  48.1 6.5 %collective-permute-start.13 = (bf16[456,128]{1,0:T(8,128)(2,1)S(1)}, bf16[456,128]{1,0:T(8,128)(2,1)S(1)}, u32[]{:S(2)}, u32[]{:S(2)}) collective-permute-start(bf16[456,128]{1,0:T(8,128)(2,1)S(1)} %get-tuple-element.39), channel_id=1, source_target_pairs={{0,16},{4,12},{8,24},{12,4},{16,0},{20,28},{24,8},{28,20},{1,17},{... | collective-permute-start | bytes 350216 | tf_op jit(solution)/shard_map/ppermute | solution.py:36
  49.6 4.5 %collective-permute-start.20 = (bf16[328,128]{1,0:T(8,128)(2,1)S(1)}, bf16[328,128]{1,0:T(8,128)(2,1)S(1)}, u32[]{:S(2)}, u32[]{:S(2)}) collective-permute-start(bf16[328,128]{1,0:T(8,128)(2,1)S(1)} %get-tuple-element.47), channel_id=1, source_target_pairs={{0,8},{4,20},{8,0},{12,28},{16,24},{20,4},{24,16},{28,12},{1,9},{5... | collective-permute-start | bytes 251912 | tf_op jit(solution)/shard_map/ppermute | solution.py:36
  50.2 4.5 %collective-permute-start.21 = (bf16[328,128]{1,0:T(8,128)(2,1)S(1)}, bf16[328,128]{1,0:T(8,128)(2,1)S(1)}, u32[]{:S(2)}, u32[]{:S(2)}) collective-permute-start(bf16[328,128]{1,0:T(8,128)(2,1)S(1)} %get-tuple-element.48), channel_id=1, source_target_pairs={{0,16},{4,12},{8,24},{12,4},{16,0},{20,28},{24,8},{28,20},{1,17},{... | collective-permute-start | bytes 251912 | tf_op jit(solution)/shard_map/ppermute | solution.py:36
  55.3 1.5 %collective-permute-start.22 = (bf16[176,640]{1,0:T(8,128)(2,1)S(1)}, bf16[176,640]{1,0:T(8,128)(2,1)S(1)}, u32[]{:S(2)}, u32[]{:S(2)}) collective-permute-start(bf16[176,640]{1,0:T(8,128)(2,1)S(1)} %get-tuple-element.51), channel_id=1, source_target_pairs={{0,4},{4,0},{8,12},{12,8},{16,20},{20,16},{24,28},{28,24},{1,5},{5... | collective-permute-start | bytes 675848 | tf_op jit(solution)/shard_map/ppermute | solution.py:36
where the time goes:
time: 57.8 us; the launch traced here: 57.7 us
  starting transfers between devices  27.8 us (48%)
  waiting for transfers between devices  23 us (40%)
  Pallas kernels  5.36 us (9%)
  between operations  1.41 us (2%)
    ppermute x6, waiting for transfers between devices, along(): return lax.ppermute(value, 'layer', pairs)  17.9 us
    ppermute x17, starting transfers between devices, swap(): return lax.ppermute(value, 'tok', pairs)  16.5 us
    ppermute x6, starting transfers between devices, along(): return lax.ppermute(value, 'layer', pairs)  11.3 us
    pallas_call x9, Pallas kernels, call(): pl.pallas_call(kernel, out_shape=outs, in_specs=specs, out_specs=[local]...  5.36 us
    ppermute x17, waiting for transfers between devices, swap(): return lax.ppermute(value, 'tok', pairs)  5.06 us
  transfers between devices with their start and end apart: 23, of which 7 were waited for; matrix products, arithmetic and copies ran while one was open for 0% of the time, Pallas kernels for 4%

commit v1 on v0

--- a/solution.py
+++ b/solution.py
@@ -167,12 +167,20 @@
         at += hi - lo
     fact = jnp.concatenate(facts, axis=1)
     scores = None
-    for (step, flip), block in zip(blocks, probes):
-        spot = pl.ds(pl.multiple_of(peer(me[0] ^ flip, step) * cols, LANES), cols)
+    spots = [
+        pl.ds(pl.multiple_of(peer(me[0] ^ flip, step) * cols, LANES), cols) for step, flip in blocks
+    ]
+    for n in range(0, len(blocks), 4):
+        members = range(n, min(n + 4, len(blocks)))
         probe = jnp.concatenate(
-            [block[piece + t * grads : piece + (t + 1) * grads, :] for t in range(tok_tiles)], axis=1
+            [
+                probes[m][piece + t * grads : piece + (t + 1) * grads, :]
+                for m in members
+                for t in range(tok_tiles)
+            ],
+            axis=1,
         )
-        part = contract(probe, rows[:, spot])
+        part = contract(probe, jnp.concatenate([rows[:, spots[m]] for m in members], axis=1))
         scores = part if scores is None else scores + part
     logits, hidden = scores[:tags], scores[tags:]
     tag_row, depth_row, count_row, place = fact[0:1], fact[1:2], fact[2:3], fact[3:4]
@@ -206,38 +214,53 @@
     return grads if folds == 1 else round_up(-(-grads // folds), 16)
 
 
-def grad_kernel(me, *refs, chips, slots, layers):
-    sets = [refs[n * chips : (n + 1) * chips] for n in range(layers)]
-    other, left, right = refs[layers * chips :]
+def gather_rows(right, at, sources, slots, tiles):
+    for p, lo, hi in spans(slots, len(sources)):
+        for t in range(tiles):
+            right[at : at + hi - lo, t * LANES : (t + 1) * LANES] = sources[p][
+                tile_rows(slots, lo, hi, t), :
+            ]
+        at += hi - lo
+    return at
+
+
+def stage_kernel(me, *refs, chips, slots, sets):
+    messages = [refs[n * chips : (n + 1) * chips] for n in range(sets)]
+    mine, other, left, right = refs[sets * chips :]
+    cols = mine.shape[1]
+    tiles = 2 * cols // LANES
+    for c in range(chips):
+        at, stop = c * LANES, (c + 1) * LANES
+        left[:, at:stop] = messages[1][c][tiles * slots :, :]
+        at = gather_rows(right, at, [part[c] for part in messages], slots, tiles)
+        if at < stop:
+            right[at:stop, :] = jnp.zeros((stop - at, 2 * cols), right.dtype)
+    core = me[0] % 2
+    mine[...] = half_grad(left, right, core, cols)
+    other[...] = half_grad(left, right, 1 - core, cols)
+
+
+def grad_kernel(me, *refs, chips, slots):
+    lates, so_far = refs[:chips], refs[chips]
+    other, left, right = refs[chips + 1 :]
     grads, cols = other.shape
     tiles = 2 * cols // LANES
-    piece = tiles * slots
-    first = (layers - 1) * slots
-    second = round_up(first, 8)
+    pad = right.shape[0] // chips
     folds = LANES // slots
+    parts = []
     for c in range(chips):
-        head = sets[1][c][piece:, :].astype(jnp.float32)
-        tail = sets[-1][c][piece:, :].astype(jnp.float32)
+        tail = lates[c][tiles * slots :, :].astype(jnp.float32)
         tail = jnp.concatenate([tail[:, n * slots : (n + 1) * slots] for n in range(folds)], axis=0)
-        both = [head[:, :second], tail[:grads]]
-        if second + slots < LANES:
-            both.append(jnp.zeros((grads, LANES - second - slots), jnp.float32))
-        at = c * LANES
-        left[:, at : at + LANES] = jnp.concatenate(both, axis=1).astype(left.dtype)
-        gaps = []
-        for start, members in ((0, range(layers - 1)), (second, range(layers - 1, layers))):
-            at = c * LANES + start
-            for p, lo, hi in spans(slots, len(members)):
-                for t in range(tiles):
-                    right[at : at + hi - lo, t * LANES : (t + 1) * LANES] = sets[members[p]][c][
-                        tile_rows(slots, lo, hi, t), :
-                    ]
-                at += hi - lo
-            gaps.append((at, c * LANES + (second if start == 0 else LANES)))
-        for lo, hi in gaps:
-            if lo < hi:
-                right[lo:hi, :] = jnp.zeros((hi - lo, 2 * cols), right.dtype)
-    other[...] = half_grad(left, right, 1 - me[0] % 2, cols).astype(other.dtype)
+        parts.append(tail[:grads])
+        at, stop = c * pad, (c + 1) * pad
+        if slots < pad:
+            parts.append(jnp.zeros((grads, pad - slots), jnp.float32))
+        at = gather_rows(right, at, [lates[c]], slots, tiles)
+        if at < stop:
+            right[at:stop, :] = jnp.zeros((stop - at, 2 * cols), right.dtype)
+    left[...] = jnp.concatenate(parts, axis=1).astype(left.dtype)
+    half = half_grad(left, right, 1 - me[0] % 2, cols)
+    other[...] = (so_far[...] + half).astype(other.dtype)
 
 
 def half_grad(left, right, half, cols):
@@ -245,8 +268,8 @@
     return jnp.dot(left[...], right[:, spot], preferred_element_type=jnp.float32)
 
 
-def mine_kernel(me, left, right, mine):
-    mine[...] = half_grad(left, right, me[0] % 2, mine.shape[1])
+def mine_kernel(me, left, right, so_far, mine):
+    mine[...] = so_far[...] + half_grad(left, right, me[0] % 2, mine.shape[1])
 
 
 def join_kernel(mine, other, pos_out, depth_out):
@@ -350,18 +373,22 @@
 
     middle = score(range(layers - 1), 1)
     late = score([layers - 1], 0)
+    part = shape((grads, cols), f32)
+    count = len(peers)
+    mine, other = call(
+        8, functools.partial(stage_kernel, chips=count, slots=slots, sets=layers - 1),
+        [part, part],
+        [pltpu.VMEM((grads, count * LANES), bf16), pltpu.VMEM((count * LANES, 2 * cols), bf16)],
+        [tok_at], *shares, *middle, *[v for values in early for v in values],
+    )
+    depth = count * round_up(slots, 16)
     other, left, right = call(
-        8,
-        functools.partial(grad_kernel, chips=len(peers), slots=slots, layers=layer_count),
-        [
-            shape((grads, cols), bf16),
-            shape((grads, len(peers) * LANES), bf16),
-            shape((len(peers) * LANES, 2 * cols), bf16),
-        ],
-        [], [tok_at], *shares, *middle, *[v for part in early for v in part], *late,
+        8, functools.partial(grad_kernel, chips=count, slots=slots),
+        [shape((grads, cols), bf16), shape((grads, depth), bf16), shape((depth, 2 * cols), bf16)],
+        [], [tok_at], *late, other,
     )
     other = swap(other, (1, 1))
-    (mine,) = call(4, mine_kernel, [shape((grads, cols), f32)], [], [tok_at], left, right)
+    (mine,) = call(4, mine_kernel, [shape((grads, cols), f32)], [], [tok_at], left, right, mine)
     return call(
         4, join_kernel,
         [shape((1, tag_count, cols), f32), shape((1, rank, cols), f32)], [], [], mine, other,

time: 57.8 us -> 54.1 us (0.936)
  waiting for transfers between devices: 23 us -> 16.8 us
  starting transfers between devices: 27.8 us -> 30.1 us
    ppermute x6, waiting for transfers between devices: 17.9 us -> 12.3 us  [along(): return lax.ppermute(value, 'layer', pairs)]
    ppermute x6, starting transfers between devices: 11.3 us -> 12.8 us  [along(): return lax.ppermute(value, 'layer', pairs)]
    ppermute x17, starting transfers between devices: 16.5 us -> 17.4 us  [swap(): return lax.ppermute(value, 'tok', pairs)]
    pallas_call x9 -> x10, Pallas kernels: 5.36 us -> 5.5 us  [call(): pl.pallas_call(kernel, out_shape=outs, in_specs=specs, out_specs=[local]...]
  transfers between devices with their start and end apart: 23 -> 23, of which waited for: 7 -> 8; matrix products, arithmetic and copies ran while one was open for 0% -> 0% of each run, Pallas kernels for 4% -> 5%
where the time goes in v1:
time: 54.1 us; the launch traced here: 54 us
  starting transfers between devices  30.1 us (56%)
  waiting for transfers between devices  16.8 us (31%)
  Pallas kernels  5.5 us (10%)
  between operations  1.42 us (3%)
    ppermute x17, starting transfers between devices, swap(): return lax.ppermute(value, 'tok', pairs)  17.4 us
    ppermute x6, starting transfers between devices, along(): return lax.ppermute(value, 'layer', pairs)  12.8 us
    ppermute x6, waiting for transfers between devices, along(): return lax.ppermute(value, 'layer', pairs)  12.3 us
    pallas_call x10, Pallas kernels, call(): pl.pallas_call(kernel, out_shape=outs, in_specs=specs, out_specs=[local]...  5.5 us
    ppermute x17, waiting for transfers between devices, swap(): return lax.ppermute(value, 'tok', pairs)  4.5 us
  transfers between devices with their start and end apart: 23, of which 8 were waited for; matrix products, arithmetic and copies ran while one was open for 0% of the time, Pallas kernels for 5%

profile of v1, /device:TPU:0, one launch (start us, length us, event | category | flops | bytes accessed | tf_op | source)
XLA Modules:
  0.0 54.0 jit_solution(16100238282495163402)
XLA Ops:
  0.7 1.4 %shard_map.80 = (bf16[1120,128]{1,0:T(8,128)(2,1)S(1)}, f32[40,112,128]{2,1,0:T(8,128)S(1)}, bf16[176,640]{1,0:T(8,128)(2,1)S(1)}) custom-call(s32[1]{0:T(128)} %bitcast.1.me, bf16[28,4,5120]{2,1,0:T(4,128)(2,1)} %bitcast.6, bf16[1,48,640]{2,1,0:T(8,128)(2,1)} %pos.1, bf16[1,128,640]{2,1,0:T(8,128)(2,1)} %depth.1), custom_call_target="tpu_custom_call" | custom-call | tf_op jit(solution)/shard_map/pallas_call | solution.py:286
  2.1 0.2 shard_map.81
  2.3 0.1 shard_map.82
  2.4 4.0 %collective-permute-start.1 = (bf16[1160,128]{1,0:T(8,128)(2,1)S(1)}, bf16[1160,128]{1,0:T(8,128)(2,1)S(1)}, u32[]{:S(2)}, u32[]{:S(2)}) collective-permute-start(bf16[1160,128]{1,0:T(8,128)(2,1)S(1)} %get-tuple-element.34), channel_id=1, source_target_pairs={{0,24},{4,28},{8,16},{12,20},{16,8},{20,12},{24,0},{28,4},{1,25},{... | collective-permute-start | bytes 890888 | tf_op jit(solution)/shard_map/ppermute | solution.py:36
  6.4 0.5 collective-permute-start.2
  7.0 0.1 collective-permute-start.3
  7.1 2.0 %collective-permute-start.12 = (bf16[1120,128]{1,0:T(8,128)(2,1)S(1)}, bf16[1120,128]{1,0:T(8,128)(2,1)S(1)}, u32[]{:S(2)}, u32[]{:S(2)}) collective-permute-start(bf16[1120,128]{1,0:T(8,128)(2,1)S(1)} %get-tuple-element.41), channel_id=1, source_target_pairs={{0,1},{1,3},{2,0},{3,2},{4,5},{5,7},{6,4},{7,6},{8,9},{9,11},{10,8... | collective-permute-start | bytes 860168 | tf_op jit(solution)/shard_map/ppermute | solution.py:319
  9.7 0.1 pad.2.clone
  9.8 0.1 pad_add_fusion.refs_11_
  9.9 2.6 %collective-permute-start.14 = (s32[4,28]{1,0:T(4,128)S(1)}, s32[4,28]{1,0:T(4,128)S(1)}, u32[]{:S(2)}, u32[]{:S(2)}) collective-permute-start(s32[4,28]{1,0:T(4,128)S(1)} %pad_add_fusion.refs_11_), channel_id=1, source_target_pairs={{0,1},{1,3},{2,0},{3,2},{4,5},{5,7},{6,4},{7,6},{8,9},{9,11},{10,8... | collective-permute-start | bytes 1352 | tf_op jit(solution)/shard_map/ppermute | solution.py:319
  12.4 3.6 %collective-permute-done.14.refs_12_ = s32[4,28]{1,0:T(4,128)S(1)} collective-permute-done((s32[4,28]{1,0:T(4,128)S(1)}, s32[4,28]{1,0:T(4,128)S(1)}, u32[]{:S(2)}, u32[]{:S(2)}) %collective-permute-start.14) | collective-permute-done | bytes 480 | tf_op jit(solution)/shard_map/ppermute | solution.py:319
  16.1 1.7 %collective-permute-start.15 = (s32[4,28]{1,0:T(4,128)S(1)}, s32[4,28]{1,0:T(4,128)S(1)}, u32[]{:S(2)}, u32[]{:S(2)}) collective-permute-start(s32[4,28]{1,0:T(4,128)S(1)} %pad_add_fusion.refs_11_), channel_id=1, source_target_pairs={{0,2},{1,0},{2,3},{3,1},{4,6},{5,4},{6,7},{7,5},{8,10},{9,8},{10,1... | collective-permute-start | bytes 1352 | tf_op jit(solution)/shard_map/ppermute | solution.py:319
  17.8 1.8 %collective-permute-done.15.refs_13_ = s32[4,28]{1,0:T(4,128)S(1)} collective-permute-done((s32[4,28]{1,0:T(4,128)S(1)}, s32[4,28]{1,0:T(4,128)S(1)}, u32[]{:S(2)}, u32[]{:S(2)}) %collective-permute-start.15) | collective-permute-done | bytes 480 | tf_op jit(solution)/shard_map/ppermute | solution.py:319
  19.7 2.6 %collective-permute-start.13 = (bf16[1120,128]{1,0:T(8,128)(2,1)S(1)}, bf16[1120,128]{1,0:T(8,128)(2,1)S(1)}, u32[]{:S(2)}, u32[]{:S(2)}) collective-permute-start(bf16[1120,128]{1,0:T(8,128)(2,1)S(1)} %get-tuple-element.42), channel_id=1, source_target_pairs={{0,2},{1,0},{2,3},{3,1},{4,6},{5,4},{6,7},{7,5},{8,10},{9,8},{10,1... | collective-permute-start | bytes 860168 | tf_op jit(solution)/shard_map/ppermute | solution.py:319
  22.3 0.0 collective-permute-done.12.refs_1_
  22.3 0.0 collective-permute-start.4
  22.3 0.0 collective-permute-done.1.refs_2_.refs_4_.refs_1_
  22.3 0.5 collective-permute-start.5
  22.8 0.0 collective-permute-done.2.refs_3_.refs_5_.refs_2_
  22.8 0.1 collective-permute-start.6
  22.9 0.4 collective-permute-start.7
  23.4 3.4 %collective-permute-done.13.refs_2_.refs_0_ = bf16[1120,128]{1,0:T(8,128)(2,1)S(1)} collective-permute-done((bf16[1120,128]{1,0:T(8,128)(2,1)S(1)}, bf16[1120,128]{1,0:T(8,128)(2,1)S(1)}, u32[]{:S(2)}, u32[]{:S(2)}) %collective-permute-start.13) | collective-permute-done | bytes 286752 | tf_op jit(solution)/shard_map/ppermute | solution.py:319
  26.8 3.2 %collective-permute-start = (bf16[1120,128]{1,0:T(8,128)(2,1)S(1)}, bf16[1120,128]{1,0:T(8,128)(2,1)S(1)}, u32[]{:S(2)}, u32[]{:S(2)}) collective-permute-start(bf16[1120,128]{1,0:T(8,128)(2,1)S(1)} %get-tuple-element.30), channel_id=1, source_target_pairs={{0,3},{1,2},{2,1},{3,0},{4,7},{5,6},{6,5},{7,4},{8,11},{9,10},{10,... | collective-permute-start | bytes 860168 | tf_op jit(solution)/shard_map/ppermute | solution.py:319
  30.0 0.0 collective-permute-done.7.refs_8_.refs_10_
  30.0 0.8 %shard_map.84 = (bf16[456,128]{1,0:T(8,128)(2,1)S(1)}, bf16[456,128]{1,0:T(8,128)(2,1)S(1)}, bf16[456,128]{1,0:T(8,128)(2,1)S(1)}, bf16[456,128]{1,0:T(8,128)(2,1)S(1)}) custom-call(s32[1]{0:T(128)} %bitcast.me, bf16[1120,128]{1,0:T(8,128)(2,1)S(1)} %get-tuple-element.31.rows.refs_0_, bf16[1120,128]{1,0:T(8,128)(2,1)S(1)} %collective-permute-done.12.refs_1_, ...), custom_call_target="tpu_custom_call" | custom-call | tf_op jit(solution)/shard_map/pallas_call | solution.py:286
  30.9 2.5 %collective-permute-start.16 = (bf16[456,128]{1,0:T(8,128)(2,1)S(1)}, bf16[456,128]{1,0:T(8,128)(2,1)S(1)}, u32[]{:S(2)}, u32[]{:S(2)}) collective-permute-start(bf16[456,128]{1,0:T(8,128)(2,1)S(1)} %get-tuple-element.44), channel_id=1, source_target_pairs={{0,24},{4,28},{8,16},{12,20},{16,8},{20,12},{24,0},{28,4},{1,25},{... | collective-permute-start | bytes 350216 | tf_op jit(solution)/shard_map/ppermute | solution.py:36
  33.4 0.5 %collective-permute-start.19 = (bf16[280,128]{1,0:T(8,128)(2,1)S(1)}, bf16[280,128]{1,0:T(8,128)(2,1)S(1)}, u32[]{:S(2)}, u32[]{:S(2)}) collective-permute-start(bf16[280,128]{1,0:T(8,128)(2,1)S(1)} %get-tuple-element.48), channel_id=1, source_target_pairs={{0,24},{4,28},{8,16},{12,20},{16,8},{20,12},{24,0},{28,4},{1,25},{... | collective-permute-start | bytes 215048 | tf_op jit(solution)/shard_map/ppermute | solution.py:36
  34.0 0.6 %collective-permute-start.8 = (s32[4,28]{1,0:T(4,128)S(1)}, s32[4,28]{1,0:T(4,128)S(1)}, u32[]{:S(2)}, u32[]{:S(2)}) collective-permute-start(s32[4,28]{1,0:T(4,128)S(1)} %pad_add_fusion.refs_11_), channel_id=1, source_target_pairs={{0,3},{1,2},{2,1},{3,0},{4,7},{5,6},{6,5},{7,4},{8,11},{9,10},{10,... | collective-permute-start | bytes 1352 | tf_op jit(solution)/shard_map/ppermute | solution.py:319
  34.5 1.5 %collective-permute-start.20 = (bf16[280,128]{1,0:T(8,128)(2,1)S(1)}, bf16[280,128]{1,0:T(8,128)(2,1)S(1)}, u32[]{:S(2)}, u32[]{:S(2)}) collective-permute-start(bf16[280,128]{1,0:T(8,128)(2,1)S(1)} %get-tuple-element.49), channel_id=1, source_target_pairs={{0,8},{4,20},{8,0},{12,28},{16,24},{20,4},{24,16},{28,12},{1,9},{5... | collective-permute-start | bytes 215048 | tf_op jit(solution)/shard_map/ppermute | solution.py:36
  36.0 3.4 %collective-permute-done.8.refs_9_ = s32[4,28]{1,0:T(4,128)S(1)} collective-permute-done((s32[4,28]{1,0:T(4,128)S(1)}, s32[4,28]{1,0:T(4,128)S(1)}, u32[]{:S(2)}, u32[]{:S(2)}) %collective-permute-start.8) | collective-permute-done | bytes 480 | tf_op jit(solution)/shard_map/ppermute | solution.py:319
  39.4 1.5 %collective-permute-start.21 = (bf16[280,128]{1,0:T(8,128)(2,1)S(1)}, bf16[280,128]{1,0:T(8,128)(2,1)S(1)}, u32[]{:S(2)}, u32[]{:S(2)}) collective-permute-start(bf16[280,128]{1,0:T(8,128)(2,1)S(1)} %get-tuple-element.50), channel_id=1, source_target_pairs={{0,16},{4,12},{8,24},{12,4},{16,0},{20,28},{24,8},{28,20},{1,17},{... | collective-permute-start | bytes 215048 | tf_op jit(solution)/shard_map/ppermute | solution.py:36
  41.0 1.5 %collective-permute-start.17 = (bf16[456,128]{1,0:T(8,128)(2,1)S(1)}, bf16[456,128]{1,0:T(8,128)(2,1)S(1)}, u32[]{:S(2)}, u32[]{:S(2)}) collective-permute-start(bf16[456,128]{1,0:T(8,128)(2,1)S(1)} %get-tuple-element.45), channel_id=1, source_target_pairs={{0,8},{4,20},{8,0},{12,28},{16,24},{20,4},{24,16},{28,12},{1,9},{5... | collective-permute-start | bytes 350216 | tf_op jit(solution)/shard_map/ppermute | solution.py:36
  42.5 0.5 collective-permute-start.18
  43.0 0.8 %shard_map.83 = (bf16[328,128]{1,0:T(8,128)(2,1)S(1)}, bf16[328,128]{1,0:T(8,128)(2,1)S(1)}, bf16[328,128]{1,0:T(8,128)(2,1)S(1)}, bf16[328,128]{1,0:T(8,128)(2,1)S(1)}) custom-call(s32[1]{0:T(128)} %bitcast.me, bf16[1120,128]{1,0:T(8,128)(2,1)S(1)} %collective-permute-done.refs_0_, bf16[1160,128]{1,0:T(8,128)(2,1)S(1)} %get-tuple-element.33.refs_1_.refs_3_.refs_0_, ...), custom_call_target="tpu_custom_call" | custom-call | tf_op jit(solution)/shard_map/pallas_call | solution.py:286
  43.7 0.0 collective-permute-done.20.refs_10_
  43.7 1.6 %collective-permute-start.9 = (bf16[328,128]{1,0:T(8,128)(2,1)S(1)}, bf16[328,128]{1,0:T(8,128)(2,1)S(1)}, u32[]{:S(2)}, u32[]{:S(2)}) collective-permute-start(bf16[328,128]{1,0:T(8,128)(2,1)S(1)} %get-tuple-element.38), channel_id=1, source_target_pairs={{0,24},{4,28},{8,16},{12,20},{16,8},{20,12},{24,0},{28,4},{1,25},{... | collective-permute-start | bytes 251912 | tf_op jit(solution)/shard_map/ppermute | solution.py:36
  45.3 1.5 %collective-permute-start.10 = (bf16[328,128]{1,0:T(8,128)(2,1)S(1)}, bf16[328,128]{1,0:T(8,128)(2,1)S(1)}, u32[]{:S(2)}, u32[]{:S(2)}) collective-permute-start(bf16[328,128]{1,0:T(8,128)(2,1)S(1)} %get-tuple-element.39), channel_id=1, source_target_pairs={{0,8},{4,20},{8,0},{12,28},{16,24},{20,4},{24,16},{28,12},{1,9},{5... | collective-permute-start | bytes 251912 | tf_op jit(solution)/shard_map/ppermute | solution.py:36
  46.8 0.0 collective-permute-done.16.refs_5_
  46.8 0.5 collective-permute-start.11
  47.3 0.7 %shard_map.86 = (f32[176,640]{1,0:T(8,128)S(1)}, f32[176,640]{1,0:T(8,128)S(1)}) custom-call(s32[1]{0:T(128)} %bitcast.me, bf16[1160,128]{1,0:T(8,128)(2,1)S(1)} %get-tuple-element.33.refs_1_.refs_3_.refs_0_, bf16[1160,128]{1,0:T(8,128)(2,1)S(1)} %collective-permute-done.1.refs_2_.refs_4_.refs_1_, ...), custom_call_target="tpu_custom_call" | custom-call | tf_op jit(solution)/shard_map/pallas_call | solution.py:286
  48.0 1.1 %collective-permute-done.9.refs_1_ = bf16[328,128]{1,0:T(8,128)(2,1)S(1)} collective-permute-done((bf16[328,128]{1,0:T(8,128)(2,1)S(1)}, bf16[328,128]{1,0:T(8,128)(2,1)S(1)}, u32[]{:S(2)}, u32[]{:S(2)}) %collective-permute-start.9) | collective-permute-done | bytes 84000 | tf_op jit(solution)/shard_map/ppermute | solution.py:36
  49.2 1.0 %collective-permute-done.10.refs_2_ = bf16[328,128]{1,0:T(8,128)(2,1)S(1)} collective-permute-done((bf16[328,128]{1,0:T(8,128)(2,1)S(1)}, bf16[328,128]{1,0:T(8,128)(2,1)S(1)}, u32[]{:S(2)}, u32[]{:S(2)}) %collective-permute-start.10) | collective-permute-done | bytes 84000 | tf_op jit(solution)/shard_map/ppermute | solution.py:36
  50.1 1.1 %collective-permute-done.11.refs_3_ = bf16[328,128]{1,0:T(8,128)(2,1)S(1)} collective-permute-done((bf16[328,128]{1,0:T(8,128)(2,1)S(1)}, bf16[328,128]{1,0:T(8,128)(2,1)S(1)}, u32[]{:S(2)}, u32[]{:S(2)}) %collective-permute-start.11) | collective-permute-done | bytes 84000 | tf_op jit(solution)/shard_map/ppermute | solution.py:36
  51.3 0.4 shard_map.87
  51.6 0.1 collective-permute-start.22
  51.7 0.2 shard_map.88.mine
  51.9 1.2 %collective-permute-done.22.other = bf16[176,640]{1,0:T(8,128)(2,1)S(1)} collective-permute-done((bf16[176,640]{1,0:T(8,128)(2,1)S(1)}, bf16[176,640]{1,0:T(8,128)(2,1)S(1)}, u32[]{:S(2)}, u32[]{:S(2)}) %collective-permute-start.22) | collective-permute-done | bytes 225312 | tf_op jit(solution)/shard_map/ppermute | solution.py:36
  53.2 0.8 %shard_map.89 = (f32[1,48,640]{2,1,0:T(8,128)}, f32[1,128,640]{2,1,0:T(8,128)}) custom-call(f32[176,640]{1,0:T(8,128)S(1)} %shard_map.88.mine, bf16[176,640]{1,0:T(8,128)(2,1)S(1)} %collective-permute-done.22.other), custom_call_target="tpu_custom_call" | custom-call | tf_op jit(solution)/shard_map/pallas_call | solution.py:286
  (15 shorter events, 0.1 us)
Async XLA Ops:
  0.6 9.2 %copy-start = (s32[28]{0:T(128)S(1)}, s32[28]{0:T(128)}, u32[]{:S(2)}) copy-start(s32[28]{0:T(128)} %param.10) | copy-start | bytes 340
  0.6 9.1 %copy-start.1 = (s32[28]{0:T(128)S(1)}, s32[28]{0:T(128)}, u32[]{:S(2)}) copy-start(s32[28]{0:T(128)} %param.9) | copy-start | bytes 340
  2.4 19.9 %collective-permute-start.1 = (bf16[1160,128]{1,0:T(8,128)(2,1)S(1)}, bf16[1160,128]{1,0:T(8,128)(2,1)S(1)}, u32[]{:S(2)}, u32[]{:S(2)}) collective-permute-start(bf16[1160,128]{1,0:T(8,128)(2,1)S(1)} %get-tuple-element.34), channel_id=1, source_target_pairs={{0,24},{4,28},{8,16},{12,20},{16,8},{20,12},{24,0},{28,4},{1,25},{... | collective-permute-start | bytes 890888 | tf_op jit(solution)/shard_map/ppermute | solution.py:36
  6.4 16.4 %collective-permute-start.2 = (bf16[1160,128]{1,0:T(8,128)(2,1)S(1)}, bf16[1160,128]{1,0:T(8,128)(2,1)S(1)}, u32[]{:S(2)}, u32[]{:S(2)}) collective-permute-start(bf16[1160,128]{1,0:T(8,128)(2,1)S(1)} %get-tuple-element.35), channel_id=1, source_target_pairs={{0,8},{4,20},{8,0},{12,28},{16,24},{20,4},{24,16},{28,12},{1,9},{5... | collective-permute-start | bytes 890888 | tf_op jit(solution)/shard_map/ppermute | solution.py:36
  7.0 16.0 %collective-permute-start.3 = (bf16[1160,128]{1,0:T(8,128)(2,1)S(1)}, bf16[1160,128]{1,0:T(8,128)(2,1)S(1)}, u32[]{:S(2)}, u32[]{:S(2)}) collective-permute-start(bf16[1160,128]{1,0:T(8,128)(2,1)S(1)} %get-tuple-element.36), channel_id=1, source_target_pairs={{0,16},{4,12},{8,24},{12,4},{16,0},{20,28},{24,8},{28,20},{1,17},{... | collective-permute-start | bytes 890888 | tf_op jit(solution)/shard_map/ppermute | solution.py:36
  7.1 15.3 %collective-permute-start.12 = (bf16[1120,128]{1,0:T(8,128)(2,1)S(1)}, bf16[1120,128]{1,0:T(8,128)(2,1)S(1)}, u32[]{:S(2)}, u32[]{:S(2)}) collective-permute-start(bf16[1120,128]{1,0:T(8,128)(2,1)S(1)} %get-tuple-element.41), channel_id=1, source_target_pairs={{0,1},{1,3},{2,0},{3,2},{4,5},{5,7},{6,4},{7,6},{8,9},{9,11},{10,8... | collective-permute-start | bytes 860168 | tf_op jit(solution)/shard_map/ppermute | solution.py:319
  9.9 6.2 %collective-permute-start.14 = (s32[4,28]{1,0:T(4,128)S(1)}, s32[4,28]{1,0:T(4,128)S(1)}, u32[]{:S(2)}, u32[]{:S(2)}) collective-permute-start(s32[4,28]{1,0:T(4,128)S(1)} %pad_add_fusion.refs_11_), channel_id=1, source_target_pairs={{0,1},{1,3},{2,0},{3,2},{4,5},{5,7},{6,4},{7,6},{8,9},{9,11},{10,8... | collective-permute-start | bytes 1352 | tf_op jit(solution)/shard_map/ppermute | solution.py:319
  16.1 3.6 %collective-permute-start.15 = (s32[4,28]{1,0:T(4,128)S(1)}, s32[4,28]{1,0:T(4,128)S(1)}, u32[]{:S(2)}, u32[]{:S(2)}) collective-permute-start(s32[4,28]{1,0:T(4,128)S(1)} %pad_add_fusion.refs_11_), channel_id=1, source_target_pairs={{0,2},{1,0},{2,3},{3,1},{4,6},{5,4},{6,7},{7,5},{8,10},{9,8},{10,1... | collective-permute-start | bytes 1352 | tf_op jit(solution)/shard_map/ppermute | solution.py:319
  19.7 7.1 %collective-permute-start.13 = (bf16[1120,128]{1,0:T(8,128)(2,1)S(1)}, bf16[1120,128]{1,0:T(8,128)(2,1)S(1)}, u32[]{:S(2)}, u32[]{:S(2)}) collective-permute-start(bf16[1120,128]{1,0:T(8,128)(2,1)S(1)} %get-tuple-element.42), channel_id=1, source_target_pairs={{0,2},{1,0},{2,3},{3,1},{4,6},{5,4},{6,7},{7,5},{8,10},{9,8},{10,1... | collective-permute-start | bytes 860168 | tf_op jit(solution)/shard_map/ppermute | solution.py:319
  22.3 7.7 %collective-permute-start.4 = (bf16[1160,128]{1,0:T(8,128)(2,1)S(1)}, bf16[1160,128]{1,0:T(8,128)(2,1)S(1)}, u32[]{:S(2)}, u32[]{:S(2)}) collective-permute-start(bf16[1160,128]{1,0:T(8,128)(2,1)S(1)} %get-tuple-element.33.refs_1_.refs_3_.refs_0_), channel_id=1, source_target_pairs={{0,4},{4,0},{8,12},{12,8},{16,20},{20,16},{24,28},{28,24},{1,5},{5... | collective-permute-start | bytes 890888 | tf_op jit(solution)/shard_map/ppermute | solution.py:36
  22.3 7.7 %collective-permute-start.5 = (bf16[1160,128]{1,0:T(8,128)(2,1)S(1)}, bf16[1160,128]{1,0:T(8,128)(2,1)S(1)}, u32[]{:S(2)}, u32[]{:S(2)}) collective-permute-start(bf16[1160,128]{1,0:T(8,128)(2,1)S(1)} %collective-permute-done.1.refs_2_.refs_4_.refs_1_), channel_id=1, source_target_pairs={{0,4},{4,0},{8,12},{12,8},{16,20},{20,16},{24,28},{28,24},{1,5},{5... | collective-permute-start | bytes 890888 | tf_op jit(solution)/shard_map/ppermute | solution.py:36
  22.8 7.2 %collective-permute-start.6 = (bf16[1160,128]{1,0:T(8,128)(2,1)S(1)}, bf16[1160,128]{1,0:T(8,128)(2,1)S(1)}, u32[]{:S(2)}, u32[]{:S(2)}) collective-permute-start(bf16[1160,128]{1,0:T(8,128)(2,1)S(1)} %collective-permute-done.2.refs_3_.refs_5_.refs_2_), channel_id=1, source_target_pairs={{0,4},{4,0},{8,12},{12,8},{16,20},{20,16},{24,28},{28,24},{1,5},{5... | collective-permute-start | bytes 890888 | tf_op jit(solution)/shard_map/ppermute | solution.py:36
  22.9 7.1 %collective-permute-start.7 = (bf16[1160,128]{1,0:T(8,128)(2,1)S(1)}, bf16[1160,128]{1,0:T(8,128)(2,1)S(1)}, u32[]{:S(2)}, u32[]{:S(2)}) collective-permute-start(bf16[1160,128]{1,0:T(8,128)(2,1)S(1)} %collective-permute-done.3.refs_4_.refs_6_.refs_3_), channel_id=1, source_target_pairs={{0,4},{4,0},{8,12},{12,8},{16,20},{20,16},{24,28},{28,24},{1,5},{5... | collective-permute-start | bytes 890888 | tf_op jit(solution)/shard_map/ppermute | solution.py:36
  26.8 14.2 %collective-permute-start = (bf16[1120,128]{1,0:T(8,128)(2,1)S(1)}, bf16[1120,128]{1,0:T(8,128)(2,1)S(1)}, u32[]{:S(2)}, u32[]{:S(2)}) collective-permute-start(bf16[1120,128]{1,0:T(8,128)(2,1)S(1)} %get-tuple-element.30), channel_id=1, source_target_pairs={{0,3},{1,2},{2,1},{3,0},{4,7},{5,6},{6,5},{7,4},{8,11},{9,10},{10,... | collective-permute-start | bytes 860168 | tf_op jit(solution)/shard_map/ppermute | solution.py:319
  30.9 15.9 %collective-permute-start.16 = (bf16[456,128]{1,0:T(8,128)(2,1)S(1)}, bf16[456,128]{1,0:T(8,128)(2,1)S(1)}, u32[]{:S(2)}, u32[]{:S(2)}) collective-permute-start(bf16[456,128]{1,0:T(8,128)(2,1)S(1)} %get-tuple-element.44), channel_id=1, source_target_pairs={{0,24},{4,28},{8,16},{12,20},{16,8},{20,12},{24,0},{28,4},{1,25},{... | collective-permute-start | bytes 350216 | tf_op jit(solution)/shard_map/ppermute | solution.py:36
  33.4 9.0 %collective-permute-start.19 = (bf16[280,128]{1,0:T(8,128)(2,1)S(1)}, bf16[280,128]{1,0:T(8,128)(2,1)S(1)}, u32[]{:S(2)}, u32[]{:S(2)}) collective-permute-start(bf16[280,128]{1,0:T(8,128)(2,1)S(1)} %get-tuple-element.48), channel_id=1, source_target_pairs={{0,24},{4,28},{8,16},{12,20},{16,8},{20,12},{24,0},{28,4},{1,25},{... | collective-permute-start | bytes 215048 | tf_op jit(solution)/shard_map/ppermute | solution.py:36
  34.0 5.5 %collective-permute-start.8 = (s32[4,28]{1,0:T(4,128)S(1)}, s32[4,28]{1,0:T(4,128)S(1)}, u32[]{:S(2)}, u32[]{:S(2)}) collective-permute-start(s32[4,28]{1,0:T(4,128)S(1)} %pad_add_fusion.refs_11_), channel_id=1, source_target_pairs={{0,3},{1,2},{2,1},{3,0},{4,7},{5,6},{6,5},{7,4},{8,11},{9,10},{10,... | collective-permute-start | bytes 1352 | tf_op jit(solution)/shard_map/ppermute | solution.py:319
  34.5 9.2 %collective-permute-start.20 = (bf16[280,128]{1,0:T(8,128)(2,1)S(1)}, bf16[280,128]{1,0:T(8,128)(2,1)S(1)}, u32[]{:S(2)}, u32[]{:S(2)}) collective-permute-start(bf16[280,128]{1,0:T(8,128)(2,1)S(1)} %get-tuple-element.49), channel_id=1, source_target_pairs={{0,8},{4,20},{8,0},{12,28},{16,24},{20,4},{24,16},{28,12},{1,9},{5... | collective-permute-start | bytes 215048 | tf_op jit(solution)/shard_map/ppermute | solution.py:36
  39.4 5.9 %collective-permute-start.21 = (bf16[280,128]{1,0:T(8,128)(2,1)S(1)}, bf16[280,128]{1,0:T(8,128)(2,1)S(1)}, u32[]{:S(2)}, u32[]{:S(2)}) collective-permute-start(bf16[280,128]{1,0:T(8,128)(2,1)S(1)} %get-tuple-element.50), channel_id=1, source_target_pairs={{0,16},{4,12},{8,24},{12,4},{16,0},{20,28},{24,8},{28,20},{1,17},{... | collective-permute-start | bytes 215048 | tf_op jit(solution)/shard_map/ppermute | solution.py:36
  41.0 6.4 %collective-permute-start.17 = (bf16[456,128]{1,0:T(8,128)(2,1)S(1)}, bf16[456,128]{1,0:T(8,128)(2,1)S(1)}, u32[]{:S(2)}, u32[]{:S(2)}) collective-permute-start(bf16[456,128]{1,0:T(8,128)(2,1)S(1)} %get-tuple-element.45), channel_id=1, source_target_pairs={{0,8},{4,20},{8,0},{12,28},{16,24},{20,4},{24,16},{28,12},{1,9},{5... | collective-permute-start | bytes 350216 | tf_op jit(solution)/shard_map/ppermute | solution.py:36
  42.5 4.9 %collective-permute-start.18 = (bf16[456,128]{1,0:T(8,128)(2,1)S(1)}, bf16[456,128]{1,0:T(8,128)(2,1)S(1)}, u32[]{:S(2)}, u32[]{:S(2)}) collective-permute-start(bf16[456,128]{1,0:T(8,128)(2,1)S(1)} %get-tuple-element.46), channel_id=1, source_target_pairs={{0,16},{4,12},{8,24},{12,4},{16,0},{20,28},{24,8},{28,20},{1,17},{... | collective-permute-start | bytes 350216 | tf_op jit(solution)/shard_map/ppermute | solution.py:36
  43.7 5.4 %collective-permute-start.9 = (bf16[328,128]{1,0:T(8,128)(2,1)S(1)}, bf16[328,128]{1,0:T(8,128)(2,1)S(1)}, u32[]{:S(2)}, u32[]{:S(2)}) collective-permute-start(bf16[328,128]{1,0:T(8,128)(2,1)S(1)} %get-tuple-element.38), channel_id=1, source_target_pairs={{0,24},{4,28},{8,16},{12,20},{16,8},{20,12},{24,0},{28,4},{1,25},{... | collective-permute-start | bytes 251912 | tf_op jit(solution)/shard_map/ppermute | solution.py:36
  45.3 4.8 %collective-permute-start.10 = (bf16[328,128]{1,0:T(8,128)(2,1)S(1)}, bf16[328,128]{1,0:T(8,128)(2,1)S(1)}, u32[]{:S(2)}, u32[]{:S(2)}) collective-permute-start(bf16[328,128]{1,0:T(8,128)(2,1)S(1)} %get-tuple-element.39), channel_id=1, source_target_pairs={{0,8},{4,20},{8,0},{12,28},{16,24},{20,4},{24,16},{28,12},{1,9},{5... | collective-permute-start | bytes 251912 | tf_op jit(solution)/shard_map/ppermute | solution.py:36
  46.8 4.5 %collective-permute-start.11 = (bf16[328,128]{1,0:T(8,128)(2,1)S(1)}, bf16[328,128]{1,0:T(8,128)(2,1)S(1)}, u32[]{:S(2)}, u32[]{:S(2)}) collective-permute-start(bf16[328,128]{1,0:T(8,128)(2,1)S(1)} %get-tuple-element.40), channel_id=1, source_target_pairs={{0,16},{4,12},{8,24},{12,4},{16,0},{20,28},{24,8},{28,20},{1,17},{... | collective-permute-start | bytes 251912 | tf_op jit(solution)/shard_map/ppermute | solution.py:36
  51.6 1.5 %collective-permute-start.22 = (bf16[176,640]{1,0:T(8,128)(2,1)S(1)}, bf16[176,640]{1,0:T(8,128)(2,1)S(1)}, u32[]{:S(2)}, u32[]{:S(2)}) collective-permute-start(bf16[176,640]{1,0:T(8,128)(2,1)S(1)} %get-tuple-element.55), channel_id=1, source_target_pairs={{0,4},{4,0},{8,12},{12,8},{16,20},{20,16},{24,28},{28,24},{1,5},{5... | collective-permute-start | bytes 675848 | tf_op jit(solution)/shard_map/ppermute | solution.py:36

commit v2 on v1

--- a/solution.py
+++ b/solution.py
@@ -272,10 +272,21 @@
     mine[...] = so_far[...] + half_grad(left, right, me[0] % 2, mine.shape[1])
 
 
-def join_kernel(mine, other, pos_out, depth_out):
-    tags = pos_out.shape[1]
-    pos_out[0] = mine[:tags] + other[:tags].astype(jnp.float32)
-    depth_out[0] = mine[tags:] + other[tags:].astype(jnp.float32)
+def join_kernel(mine, other, pos_out, depth_out, held, sems):
+    tags, rank = pos_out.shape[1], depth_out.shape[1]
+    half = rank // 2
+    parts = [
+        (0, tags, pos_out.at[0]),
+        (tags, tags + half, depth_out.at[0, :half]),
+        (tags + half, tags + rank, depth_out.at[0, half:]),
+    ]
+    copies = []
+    for n, (lo, hi, target) in enumerate(parts):
+        held[lo:hi, :] = mine[lo:hi, :] + other[lo:hi, :].astype(jnp.float32)
+        copies.append(pltpu.make_async_copy(held.at[lo:hi], target, sems.at[n]))
+        copies[-1].start()
+    for copy in copies:
+        copy.wait()
 
 
 def call(vmem, kernel, outs, scratch, scalars, *values, spaces=()):
@@ -389,10 +400,16 @@
     )
     other = swap(other, (1, 1))
     (mine,) = call(4, mine_kernel, [shape((grads, cols), f32)], [], [tok_at], left, right, mine)
-    return call(
-        4, join_kernel,
-        [shape((1, tag_count, cols), f32), shape((1, rank, cols), f32)], [], [], mine, other,
-    )
+    local_space, far = pl.BlockSpec(memory_space=pltpu.VMEM), pl.BlockSpec(memory_space=pltpu.HBM)
+    return pl.pallas_call(
+        join_kernel,
+        out_shape=[shape((1, tag_count, cols), f32), shape((1, rank, cols), f32)],
+        in_specs=[local_space] * 2,
+        out_specs=[far] * 2,
+        scratch_shapes=[pltpu.VMEM((grads, cols), f32), pltpu.SemaphoreType.DMA((3,))],
+        compiler_params=pltpu.CompilerParams(vmem_limit_bytes=4 << 20),
+        name="join",
+    )(mine, other)
 
 
 def general(activations, pos_weight, depth_weight, tags, depths, counts):

time: 54.1 us -> 54.1 us (level)
    pallas_call x10 -> x9, Pallas kernels: 5.5 us -> 4.68 us  [call(): pl.pallas_call(kernel, out_shape=outs, in_specs=specs, out_specs=[local]...]
    pallas_call x0 -> x1, Pallas kernels: none -> 0.8 us  [fast(): pl.pallas_call(join_kernel, out_shape=[shape((1, tag_count, cols), f32),...]
where the time goes in v2:
time: 54.1 us; the launch traced here: 54 us
  starting transfers between devices  30.1 us (56%)
  waiting for transfers between devices  16.8 us (31%)
  Pallas kernels  5.48 us (10%)
  between operations  1.42 us (3%)
    ppermute x17, starting transfers between devices, swap(): return lax.ppermute(value, 'tok', pairs)  17.4 us
    ppermute x6, starting transfers between devices, along(): return lax.ppermute(value, 'layer', pairs)  12.8 us
    ppermute x6, waiting for transfers between devices, along(): return lax.ppermute(value, 'layer', pairs)  12.3 us
    pallas_call x9, Pallas kernels, call(): pl.pallas_call(kernel, out_shape=outs, in_specs=specs, out_specs=[local]...  4.68 us
    ppermute x17, waiting for transfers between devices, swap(): return lax.ppermute(value, 'tok', pairs)  4.5 us
  transfers between devices with their start and end apart: 23, of which 8 were waited for; matrix products, arithmetic and copies ran while one was open for 0% of the time, Pallas kernels for 5%

profile of v2, /device:TPU:0, one launch (start us, length us, event | category | flops | bytes accessed | tf_op | source)
XLA Modules:
  0.0 54.0 jit_solution(11383535901696619823)
XLA Ops:
  0.7 1.4 %shard_map.80 = (bf16[1120,128]{1,0:T(8,128)(2,1)S(1)}, f32[40,112,128]{2,1,0:T(8,128)S(1)}, bf16[176,640]{1,0:T(8,128)(2,1)S(1)}) custom-call(s32[1]{0:T(128)} %bitcast.1.me, bf16[28,4,5120]{2,1,0:T(4,128)(2,1)} %bitcast.6, bf16[1,48,640]{2,1,0:T(8,128)(2,1)} %pos.1, bf16[1,128,640]{2,1,0:T(8,128)(2,1)} %depth.1), custom_call_target="tpu_custom_call" | custom-call | tf_op jit(solution)/shard_map/pallas_call | solution.py:297
  2.1 0.2 shard_map.81
  2.3 0.1 shard_map.82
  2.4 4.0 %collective-permute-start.1 = (bf16[1160,128]{1,0:T(8,128)(2,1)S(1)}, bf16[1160,128]{1,0:T(8,128)(2,1)S(1)}, u32[]{:S(2)}, u32[]{:S(2)}) collective-permute-start(bf16[1160,128]{1,0:T(8,128)(2,1)S(1)} %get-tuple-element.34), channel_id=1, source_target_pairs={{0,24},{4,28},{8,16},{12,20},{16,8},{20,12},{24,0},{28,4},{1,25},{... | collective-permute-start | bytes 890888 | tf_op jit(solution)/shard_map/ppermute | solution.py:36
  6.4 0.5 collective-permute-start.2
  7.0 0.1 collective-permute-start.3
  7.1 2.0 %collective-permute-start.12 = (bf16[1120,128]{1,0:T(8,128)(2,1)S(1)}, bf16[1120,128]{1,0:T(8,128)(2,1)S(1)}, u32[]{:S(2)}, u32[]{:S(2)}) collective-permute-start(bf16[1120,128]{1,0:T(8,128)(2,1)S(1)} %get-tuple-element.41), channel_id=1, source_target_pairs={{0,1},{1,3},{2,0},{3,2},{4,5},{5,7},{6,4},{7,6},{8,9},{9,11},{10,8... | collective-permute-start | bytes 860168 | tf_op jit(solution)/shard_map/ppermute | solution.py:330
  9.7 0.1 pad.2.clone
  9.8 0.1 pad_add_fusion.refs_11_
  9.9 2.6 %collective-permute-start.14 = (s32[4,28]{1,0:T(4,128)S(1)}, s32[4,28]{1,0:T(4,128)S(1)}, u32[]{:S(2)}, u32[]{:S(2)}) collective-permute-start(s32[4,28]{1,0:T(4,128)S(1)} %pad_add_fusion.refs_11_), channel_id=1, source_target_pairs={{0,1},{1,3},{2,0},{3,2},{4,5},{5,7},{6,4},{7,6},{8,9},{9,11},{10,8... | collective-permute-start | bytes 1352 | tf_op jit(solution)/shard_map/ppermute | solution.py:330
  12.4 3.6 %collective-permute-done.14.refs_12_ = s32[4,28]{1,0:T(4,128)S(1)} collective-permute-done((s32[4,28]{1,0:T(4,128)S(1)}, s32[4,28]{1,0:T(4,128)S(1)}, u32[]{:S(2)}, u32[]{:S(2)}) %collective-permute-start.14) | collective-permute-done | bytes 480 | tf_op jit(solution)/shard_map/ppermute | solution.py:330
  16.1 1.7 %collective-permute-start.15 = (s32[4,28]{1,0:T(4,128)S(1)}, s32[4,28]{1,0:T(4,128)S(1)}, u32[]{:S(2)}, u32[]{:S(2)}) collective-permute-start(s32[4,28]{1,0:T(4,128)S(1)} %pad_add_fusion.refs_11_), channel_id=1, source_target_pairs={{0,2},{1,0},{2,3},{3,1},{4,6},{5,4},{6,7},{7,5},{8,10},{9,8},{10,1... | collective-permute-start | bytes 1352 | tf_op jit(solution)/shard_map/ppermute | solution.py:330
  17.8 1.8 %collective-permute-done.15.refs_13_ = s32[4,28]{1,0:T(4,128)S(1)} collective-permute-done((s32[4,28]{1,0:T(4,128)S(1)}, s32[4,28]{1,0:T(4,128)S(1)}, u32[]{:S(2)}, u32[]{:S(2)}) %collective-permute-start.15) | collective-permute-done | bytes 480 | tf_op jit(solution)/shard_map/ppermute | solution.py:330
  19.7 2.6 %collective-permute-start.13 = (bf16[1120,128]{1,0:T(8,128)(2,1)S(1)}, bf16[1120,128]{1,0:T(8,128)(2,1)S(1)}, u32[]{:S(2)}, u32[]{:S(2)}) collective-permute-start(bf16[1120,128]{1,0:T(8,128)(2,1)S(1)} %get-tuple-element.42), channel_id=1, source_target_pairs={{0,2},{1,0},{2,3},{3,1},{4,6},{5,4},{6,7},{7,5},{8,10},{9,8},{10,1... | collective-permute-start | bytes 860168 | tf_op jit(solution)/shard_map/ppermute | solution.py:330
  22.3 0.0 collective-permute-done.12.refs_1_
  22.3 0.0 collective-permute-start.4
  22.3 0.0 collective-permute-done.1.refs_2_.refs_4_.refs_1_
  22.3 0.5 collective-permute-start.5
  22.8 0.0 collective-permute-done.2.refs_3_.refs_5_.refs_2_
  22.8 0.1 collective-permute-start.6
  22.9 0.4 collective-permute-start.7
  23.4 3.4 %collective-permute-done.13.refs_2_.refs_0_ = bf16[1120,128]{1,0:T(8,128)(2,1)S(1)} collective-permute-done((bf16[1120,128]{1,0:T(8,128)(2,1)S(1)}, bf16[1120,128]{1,0:T(8,128)(2,1)S(1)}, u32[]{:S(2)}, u32[]{:S(2)}) %collective-permute-start.13) | collective-permute-done | bytes 286752 | tf_op jit(solution)/shard_map/ppermute | solution.py:330
  26.8 3.2 %collective-permute-start = (bf16[1120,128]{1,0:T(8,128)(2,1)S(1)}, bf16[1120,128]{1,0:T(8,128)(2,1)S(1)}, u32[]{:S(2)}, u32[]{:S(2)}) collective-permute-start(bf16[1120,128]{1,0:T(8,128)(2,1)S(1)} %get-tuple-element.30), channel_id=1, source_target_pairs={{0,3},{1,2},{2,1},{3,0},{4,7},{5,6},{6,5},{7,4},{8,11},{9,10},{10,... | collective-permute-start | bytes 860168 | tf_op jit(solution)/shard_map/ppermute | solution.py:330
  30.0 0.0 collective-permute-done.7.refs_8_.refs_10_
  30.0 0.8 %shard_map.84 = (bf16[456,128]{1,0:T(8,128)(2,1)S(1)}, bf16[456,128]{1,0:T(8,128)(2,1)S(1)}, bf16[456,128]{1,0:T(8,128)(2,1)S(1)}, bf16[456,128]{1,0:T(8,128)(2,1)S(1)}) custom-call(s32[1]{0:T(128)} %bitcast.me, bf16[1120,128]{1,0:T(8,128)(2,1)S(1)} %get-tuple-element.31.rows.refs_0_, bf16[1120,128]{1,0:T(8,128)(2,1)S(1)} %collective-permute-done.12.refs_1_, ...), custom_call_target="tpu_custom_call" | custom-call | tf_op jit(solution)/shard_map/pallas_call | solution.py:297
  30.9 2.5 %collective-permute-start.16 = (bf16[456,128]{1,0:T(8,128)(2,1)S(1)}, bf16[456,128]{1,0:T(8,128)(2,1)S(1)}, u32[]{:S(2)}, u32[]{:S(2)}) collective-permute-start(bf16[456,128]{1,0:T(8,128)(2,1)S(1)} %get-tuple-element.44), channel_id=1, source_target_pairs={{0,24},{4,28},{8,16},{12,20},{16,8},{20,12},{24,0},{28,4},{1,25},{... | collective-permute-start | bytes 350216 | tf_op jit(solution)/shard_map/ppermute | solution.py:36
  33.4 0.5 %collective-permute-start.19 = (bf16[280,128]{1,0:T(8,128)(2,1)S(1)}, bf16[280,128]{1,0:T(8,128)(2,1)S(1)}, u32[]{:S(2)}, u32[]{:S(2)}) collective-permute-start(bf16[280,128]{1,0:T(8,128)(2,1)S(1)} %get-tuple-element.48), channel_id=1, source_target_pairs={{0,24},{4,28},{8,16},{12,20},{16,8},{20,12},{24,0},{28,4},{1,25},{... | collective-permute-start | bytes 215048 | tf_op jit(solution)/shard_map/ppermute | solution.py:36
  34.0 0.6 %collective-permute-start.8 = (s32[4,28]{1,0:T(4,128)S(1)}, s32[4,28]{1,0:T(4,128)S(1)}, u32[]{:S(2)}, u32[]{:S(2)}) collective-permute-start(s32[4,28]{1,0:T(4,128)S(1)} %pad_add_fusion.refs_11_), channel_id=1, source_target_pairs={{0,3},{1,2},{2,1},{3,0},{4,7},{5,6},{6,5},{7,4},{8,11},{9,10},{10,... | collective-permute-start | bytes 1352 | tf_op jit(solution)/shard_map/ppermute | solution.py:330
  34.5 1.5 %collective-permute-start.20 = (bf16[280,128]{1,0:T(8,128)(2,1)S(1)}, bf16[280,128]{1,0:T(8,128)(2,1)S(1)}, u32[]{:S(2)}, u32[]{:S(2)}) collective-permute-start(bf16[280,128]{1,0:T(8,128)(2,1)S(1)} %get-tuple-element.49), channel_id=1, source_target_pairs={{0,8},{4,20},{8,0},{12,28},{16,24},{20,4},{24,16},{28,12},{1,9},{5... | collective-permute-start | bytes 215048 | tf_op jit(solution)/shard_map/ppermute | solution.py:36
  36.0 3.4 %collective-permute-done.8.refs_9_ = s32[4,28]{1,0:T(4,128)S(1)} collective-permute-done((s32[4,28]{1,0:T(4,128)S(1)}, s32[4,28]{1,0:T(4,128)S(1)}, u32[]{:S(2)}, u32[]{:S(2)}) %collective-permute-start.8) | collective-permute-done | bytes 480 | tf_op jit(solution)/shard_map/ppermute | solution.py:330
  39.4 1.5 %collective-permute-start.21 = (bf16[280,128]{1,0:T(8,128)(2,1)S(1)}, bf16[280,128]{1,0:T(8,128)(2,1)S(1)}, u32[]{:S(2)}, u32[]{:S(2)}) collective-permute-start(bf16[280,128]{1,0:T(8,128)(2,1)S(1)} %get-tuple-element.50), channel_id=1, source_target_pairs={{0,16},{4,12},{8,24},{12,4},{16,0},{20,28},{24,8},{28,20},{1,17},{... | collective-permute-start | bytes 215048 | tf_op jit(solution)/shard_map/ppermute | solution.py:36
  41.0 1.5 %collective-permute-start.17 = (bf16[456,128]{1,0:T(8,128)(2,1)S(1)}, bf16[456,128]{1,0:T(8,128)(2,1)S(1)}, u32[]{:S(2)}, u32[]{:S(2)}) collective-permute-start(bf16[456,128]{1,0:T(8,128)(2,1)S(1)} %get-tuple-element.45), channel_id=1, source_target_pairs={{0,8},{4,20},{8,0},{12,28},{16,24},{20,4},{24,16},{28,12},{1,9},{5... | collective-permute-start | bytes 350216 | tf_op jit(solution)/shard_map/ppermute | solution.py:36
  42.5 0.5 collective-permute-start.18
  43.0 0.8 %shard_map.83 = (bf16[328,128]{1,0:T(8,128)(2,1)S(1)}, bf16[328,128]{1,0:T(8,128)(2,1)S(1)}, bf16[328,128]{1,0:T(8,128)(2,1)S(1)}, bf16[328,128]{1,0:T(8,128)(2,1)S(1)}) custom-call(s32[1]{0:T(128)} %bitcast.me, bf16[1120,128]{1,0:T(8,128)(2,1)S(1)} %collective-permute-done.refs_0_, bf16[1160,128]{1,0:T(8,128)(2,1)S(1)} %get-tuple-element.33.refs_1_.refs_3_.refs_0_, ...), custom_call_target="tpu_custom_call" | custom-call | tf_op jit(solution)/shard_map/pallas_call | solution.py:297
  43.7 0.0 collective-permute-done.20.refs_10_
  43.7 1.6 %collective-permute-start.9 = (bf16[328,128]{1,0:T(8,128)(2,1)S(1)}, bf16[328,128]{1,0:T(8,128)(2,1)S(1)}, u32[]{:S(2)}, u32[]{:S(2)}) collective-permute-start(bf16[328,128]{1,0:T(8,128)(2,1)S(1)} %get-tuple-element.38), channel_id=1, source_target_pairs={{0,24},{4,28},{8,16},{12,20},{16,8},{20,12},{24,0},{28,4},{1,25},{... | collective-permute-start | bytes 251912 | tf_op jit(solution)/shard_map/ppermute | solution.py:36
  45.3 1.5 %collective-permute-start.10 = (bf16[328,128]{1,0:T(8,128)(2,1)S(1)}, bf16[328,128]{1,0:T(8,128)(2,1)S(1)}, u32[]{:S(2)}, u32[]{:S(2)}) collective-permute-start(bf16[328,128]{1,0:T(8,128)(2,1)S(1)} %get-tuple-element.39), channel_id=1, source_target_pairs={{0,8},{4,20},{8,0},{12,28},{16,24},{20,4},{24,16},{28,12},{1,9},{5... | collective-permute-start | bytes 251912 | tf_op jit(solution)/shard_map/ppermute | solution.py:36
  46.8 0.0 collective-permute-done.16.refs_5_
  46.8 0.5 collective-permute-start.11
  47.3 0.7 %shard_map.86 = (f32[176,640]{1,0:T(8,128)S(1)}, f32[176,640]{1,0:T(8,128)S(1)}) custom-call(s32[1]{0:T(128)} %bitcast.me, bf16[1160,128]{1,0:T(8,128)(2,1)S(1)} %get-tuple-element.33.refs_1_.refs_3_.refs_0_, bf16[1160,128]{1,0:T(8,128)(2,1)S(1)} %collective-permute-done.1.refs_2_.refs_4_.refs_1_, ...), custom_call_target="tpu_custom_call" | custom-call | tf_op jit(solution)/shard_map/pallas_call | solution.py:297
  48.0 1.1 %collective-permute-done.9.refs_1_ = bf16[328,128]{1,0:T(8,128)(2,1)S(1)} collective-permute-done((bf16[328,128]{1,0:T(8,128)(2,1)S(1)}, bf16[328,128]{1,0:T(8,128)(2,1)S(1)}, u32[]{:S(2)}, u32[]{:S(2)}) %collective-permute-start.9) | collective-permute-done | bytes 84000 | tf_op jit(solution)/shard_map/ppermute | solution.py:36
  49.2 1.0 %collective-permute-done.10.refs_2_ = bf16[328,128]{1,0:T(8,128)(2,1)S(1)} collective-permute-done((bf16[328,128]{1,0:T(8,128)(2,1)S(1)}, bf16[328,128]{1,0:T(8,128)(2,1)S(1)}, u32[]{:S(2)}, u32[]{:S(2)}) %collective-permute-start.10) | collective-permute-done | bytes 84000 | tf_op jit(solution)/shard_map/ppermute | solution.py:36
  50.1 1.1 %collective-permute-done.11.refs_3_ = bf16[328,128]{1,0:T(8,128)(2,1)S(1)} collective-permute-done((bf16[328,128]{1,0:T(8,128)(2,1)S(1)}, bf16[328,128]{1,0:T(8,128)(2,1)S(1)}, u32[]{:S(2)}, u32[]{:S(2)}) %collective-permute-start.11) | collective-permute-done | bytes 84000 | tf_op jit(solution)/shard_map/ppermute | solution.py:36
  51.3 0.4 shard_map.87
  51.6 0.1 collective-permute-start.22
  51.7 0.2 shard_map.88.mine
  51.9 1.2 %collective-permute-done.22.other = bf16[176,640]{1,0:T(8,128)(2,1)S(1)} collective-permute-done((bf16[176,640]{1,0:T(8,128)(2,1)S(1)}, bf16[176,640]{1,0:T(8,128)(2,1)S(1)}, u32[]{:S(2)}, u32[]{:S(2)}) %collective-permute-start.22) | collective-permute-done | bytes 225312 | tf_op jit(solution)/shard_map/ppermute | solution.py:36
  53.2 0.8 %join.1 = (f32[1,48,640]{2,1,0:T(8,128)}, f32[1,128,640]{2,1,0:T(8,128)}) custom-call(f32[176,640]{1,0:T(8,128)S(1)} %shard_map.88.mine, bf16[176,640]{1,0:T(8,128)(2,1)S(1)} %collective-permute-done.22.other), custom_call_target="tpu_custom_call" | custom-call | tf_op jit(solution)/shard_map/join/pallas_call | solution.py:404
  (15 shorter events, 0.1 us)
Async XLA Ops:
  0.6 9.2 %copy-start = (s32[28]{0:T(128)S(1)}, s32[28]{0:T(128)}, u32[]{:S(2)}) copy-start(s32[28]{0:T(128)} %param.10) | copy-start | bytes 340
  0.6 9.1 %copy-start.1 = (s32[28]{0:T(128)S(1)}, s32[28]{0:T(128)}, u32[]{:S(2)}) copy-start(s32[28]{0:T(128)} %param.9) | copy-start | bytes 340
  2.4 19.9 %collective-permute-start.1 = (bf16[1160,128]{1,0:T(8,128)(2,1)S(1)}, bf16[1160,128]{1,0:T(8,128)(2,1)S(1)}, u32[]{:S(2)}, u32[]{:S(2)}) collective-permute-start(bf16[1160,128]{1,0:T(8,128)(2,1)S(1)} %get-tuple-element.34), channel_id=1, source_target_pairs={{0,24},{4,28},{8,16},{12,20},{16,8},{20,12},{24,0},{28,4},{1,25},{... | collective-permute-start | bytes 890888 | tf_op jit(solution)/shard_map/ppermute | solution.py:36
  6.4 16.4 %collective-permute-start.2 = (bf16[1160,128]{1,0:T(8,128)(2,1)S(1)}, bf16[1160,128]{1,0:T(8,128)(2,1)S(1)}, u32[]{:S(2)}, u32[]{:S(2)}) collective-permute-start(bf16[1160,128]{1,0:T(8,128)(2,1)S(1)} %get-tuple-element.35), channel_id=1, source_target_pairs={{0,8},{4,20},{8,0},{12,28},{16,24},{20,4},{24,16},{28,12},{1,9},{5... | collective-permute-start | bytes 890888 | tf_op jit(solution)/shard_map/ppermute | solution.py:36
  7.0 16.0 %collective-permute-start.3 = (bf16[1160,128]{1,0:T(8,128)(2,1)S(1)}, bf16[1160,128]{1,0:T(8,128)(2,1)S(1)}, u32[]{:S(2)}, u32[]{:S(2)}) collective-permute-start(bf16[1160,128]{1,0:T(8,128)(2,1)S(1)} %get-tuple-element.36), channel_id=1, source_target_pairs={{0,16},{4,12},{8,24},{12,4},{16,0},{20,28},{24,8},{28,20},{1,17},{... | collective-permute-start | bytes 890888 | tf_op jit(solution)/shard_map/ppermute | solution.py:36
  7.1 15.3 %collective-permute-start.12 = (bf16[1120,128]{1,0:T(8,128)(2,1)S(1)}, bf16[1120,128]{1,0:T(8,128)(2,1)S(1)}, u32[]{:S(2)}, u32[]{:S(2)}) collective-permute-start(bf16[1120,128]{1,0:T(8,128)(2,1)S(1)} %get-tuple-element.41), channel_id=1, source_target_pairs={{0,1},{1,3},{2,0},{3,2},{4,5},{5,7},{6,4},{7,6},{8,9},{9,11},{10,8... | collective-permute-start | bytes 860168 | tf_op jit(solution)/shard_map/ppermute | solution.py:330
  9.9 6.2 %collective-permute-start.14 = (s32[4,28]{1,0:T(4,128)S(1)}, s32[4,28]{1,0:T(4,128)S(1)}, u32[]{:S(2)}, u32[]{:S(2)}) collective-permute-start(s32[4,28]{1,0:T(4,128)S(1)} %pad_add_fusion.refs_11_), channel_id=1, source_target_pairs={{0,1},{1,3},{2,0},{3,2},{4,5},{5,7},{6,4},{7,6},{8,9},{9,11},{10,8... | collective-permute-start | bytes 1352 | tf_op jit(solution)/shard_map/ppermute | solution.py:330
  16.1 3.6 %collective-permute-start.15 = (s32[4,28]{1,0:T(4,128)S(1)}, s32[4,28]{1,0:T(4,128)S(1)}, u32[]{:S(2)}, u32[]{:S(2)}) collective-permute-start(s32[4,28]{1,0:T(4,128)S(1)} %pad_add_fusion.refs_11_), channel_id=1, source_target_pairs={{0,2},{1,0},{2,3},{3,1},{4,6},{5,4},{6,7},{7,5},{8,10},{9,8},{10,1... | collective-permute-start | bytes 1352 | tf_op jit(solution)/shard_map/ppermute | solution.py:330
  19.7 7.1 %collective-permute-start.13 = (bf16[1120,128]{1,0:T(8,128)(2,1)S(1)}, bf16[1120,128]{1,0:T(8,128)(2,1)S(1)}, u32[]{:S(2)}, u32[]{:S(2)}) collective-permute-start(bf16[1120,128]{1,0:T(8,128)(2,1)S(1)} %get-tuple-element.42), channel_id=1, source_target_pairs={{0,2},{1,0},{2,3},{3,1},{4,6},{5,4},{6,7},{7,5},{8,10},{9,8},{10,1... | collective-permute-start | bytes 860168 | tf_op jit(solution)/shard_map/ppermute | solution.py:330
  22.3 7.7 %collective-permute-start.4 = (bf16[1160,128]{1,0:T(8,128)(2,1)S(1)}, bf16[1160,128]{1,0:T(8,128)(2,1)S(1)}, u32[]{:S(2)}, u32[]{:S(2)}) collective-permute-start(bf16[1160,128]{1,0:T(8,128)(2,1)S(1)} %get-tuple-element.33.refs_1_.refs_3_.refs_0_), channel_id=1, source_target_pairs={{0,4},{4,0},{8,12},{12,8},{16,20},{20,16},{24,28},{28,24},{1,5},{5... | collective-permute-start | bytes 890888 | tf_op jit(solution)/shard_map/ppermute | solution.py:36
  22.3 7.7 %collective-permute-start.5 = (bf16[1160,128]{1,0:T(8,128)(2,1)S(1)}, bf16[1160,128]{1,0:T(8,128)(2,1)S(1)}, u32[]{:S(2)}, u32[]{:S(2)}) collective-permute-start(bf16[1160,128]{1,0:T(8,128)(2,1)S(1)} %collective-permute-done.1.refs_2_.refs_4_.refs_1_), channel_id=1, source_target_pairs={{0,4},{4,0},{8,12},{12,8},{16,20},{20,16},{24,28},{28,24},{1,5},{5... | collective-permute-start | bytes 890888 | tf_op jit(solution)/shard_map/ppermute | solution.py:36
  22.8 7.2 %collective-permute-start.6 = (bf16[1160,128]{1,0:T(8,128)(2,1)S(1)}, bf16[1160,128]{1,0:T(8,128)(2,1)S(1)}, u32[]{:S(2)}, u32[]{:S(2)}) collective-permute-start(bf16[1160,128]{1,0:T(8,128)(2,1)S(1)} %collective-permute-done.2.refs_3_.refs_5_.refs_2_), channel_id=1, source_target_pairs={{0,4},{4,0},{8,12},{12,8},{16,20},{20,16},{24,28},{28,24},{1,5},{5... | collective-permute-start | bytes 890888 | tf_op jit(solution)/shard_map/ppermute | solution.py:36
  22.9 7.1 %collective-permute-start.7 = (bf16[1160,128]{1,0:T(8,128)(2,1)S(1)}, bf16[1160,128]{1,0:T(8,128)(2,1)S(1)}, u32[]{:S(2)}, u32[]{:S(2)}) collective-permute-start(bf16[1160,128]{1,0:T(8,128)(2,1)S(1)} %collective-permute-done.3.refs_4_.refs_6_.refs_3_), channel_id=1, source_target_pairs={{0,4},{4,0},{8,12},{12,8},{16,20},{20,16},{24,28},{28,24},{1,5},{5... | collective-permute-start | bytes 890888 | tf_op jit(solution)/shard_map/ppermute | solution.py:36
  26.8 14.2 %collective-permute-start = (bf16[1120,128]{1,0:T(8,128)(2,1)S(1)}, bf16[1120,128]{1,0:T(8,128)(2,1)S(1)}, u32[]{:S(2)}, u32[]{:S(2)}) collective-permute-start(bf16[1120,128]{1,0:T(8,128)(2,1)S(1)} %get-tuple-element.30), channel_id=1, source_target_pairs={{0,3},{1,2},{2,1},{3,0},{4,7},{5,6},{6,5},{7,4},{8,11},{9,10},{10,... | collective-permute-start | bytes 860168 | tf_op jit(solution)/shard_map/ppermute | solution.py:330
  30.9 15.9 %collective-permute-start.16 = (bf16[456,128]{1,0:T(8,128)(2,1)S(1)}, bf16[456,128]{1,0:T(8,128)(2,1)S(1)}, u32[]{:S(2)}, u32[]{:S(2)}) collective-permute-start(bf16[456,128]{1,0:T(8,128)(2,1)S(1)} %get-tuple-element.44), channel_id=1, source_target_pairs={{0,24},{4,28},{8,16},{12,20},{16,8},{20,12},{24,0},{28,4},{1,25},{... | collective-permute-start | bytes 350216 | tf_op jit(solution)/shard_map/ppermute | solution.py:36
  33.4 9.0 %collective-permute-start.19 = (bf16[280,128]{1,0:T(8,128)(2,1)S(1)}, bf16[280,128]{1,0:T(8,128)(2,1)S(1)}, u32[]{:S(2)}, u32[]{:S(2)}) collective-permute-start(bf16[280,128]{1,0:T(8,128)(2,1)S(1)} %get-tuple-element.48), channel_id=1, source_target_pairs={{0,24},{4,28},{8,16},{12,20},{16,8},{20,12},{24,0},{28,4},{1,25},{... | collective-permute-start | bytes 215048 | tf_op jit(solution)/shard_map/ppermute | solution.py:36
  34.0 5.5 %collective-permute-start.8 = (s32[4,28]{1,0:T(4,128)S(1)}, s32[4,28]{1,0:T(4,128)S(1)}, u32[]{:S(2)}, u32[]{:S(2)}) collective-permute-start(s32[4,28]{1,0:T(4,128)S(1)} %pad_add_fusion.refs_11_), channel_id=1, source_target_pairs={{0,3},{1,2},{2,1},{3,0},{4,7},{5,6},{6,5},{7,4},{8,11},{9,10},{10,... | collective-permute-start | bytes 1352 | tf_op jit(solution)/shard_map/ppermute | solution.py:330
  34.5 9.2 %collective-permute-start.20 = (bf16[280,128]{1,0:T(8,128)(2,1)S(1)}, bf16[280,128]{1,0:T(8,128)(2,1)S(1)}, u32[]{:S(2)}, u32[]{:S(2)}) collective-permute-start(bf16[280,128]{1,0:T(8,128)(2,1)S(1)} %get-tuple-element.49), channel_id=1, source_target_pairs={{0,8},{4,20},{8,0},{12,28},{16,24},{20,4},{24,16},{28,12},{1,9},{5... | collective-permute-start | bytes 215048 | tf_op jit(solution)/shard_map/ppermute | solution.py:36
  39.4 5.9 %collective-permute-start.21 = (bf16[280,128]{1,0:T(8,128)(2,1)S(1)}, bf16[280,128]{1,0:T(8,128)(2,1)S(1)}, u32[]{:S(2)}, u32[]{:S(2)}) collective-permute-start(bf16[280,128]{1,0:T(8,128)(2,1)S(1)} %get-tuple-element.50), channel_id=1, source_target_pairs={{0,16},{4,12},{8,24},{12,4},{16,0},{20,28},{24,8},{28,20},{1,17},{... | collective-permute-start | bytes 215048 | tf_op jit(solution)/shard_map/ppermute | solution.py:36
  41.0 6.4 %collective-permute-start.17 = (bf16[456,128]{1,0:T(8,128)(2,1)S(1)}, bf16[456,128]{1,0:T(8,128)(2,1)S(1)}, u32[]{:S(2)}, u32[]{:S(2)}) collective-permute-start(bf16[456,128]{1,0:T(8,128)(2,1)S(1)} %get-tuple-element.45), channel_id=1, source_target_pairs={{0,8},{4,20},{8,0},{12,28},{16,24},{20,4},{24,16},{28,12},{1,9},{5... | collective-permute-start | bytes 350216 | tf_op jit(solution)/shard_map/ppermute | solution.py:36
  42.5 4.9 %collective-permute-start.18 = (bf16[456,128]{1,0:T(8,128)(2,1)S(1)}, bf16[456,128]{1,0:T(8,128)(2,1)S(1)}, u32[]{:S(2)}, u32[]{:S(2)}) collective-permute-start(bf16[456,128]{1,0:T(8,128)(2,1)S(1)} %get-tuple-element.46), channel_id=1, source_target_pairs={{0,16},{4,12},{8,24},{12,4},{16,0},{20,28},{24,8},{28,20},{1,17},{... | collective-permute-start | bytes 350216 | tf_op jit(solution)/shard_map/ppermute | solution.py:36
  43.7 5.4 %collective-permute-start.9 = (bf16[328,128]{1,0:T(8,128)(2,1)S(1)}, bf16[328,128]{1,0:T(8,128)(2,1)S(1)}, u32[]{:S(2)}, u32[]{:S(2)}) collective-permute-start(bf16[328,128]{1,0:T(8,128)(2,1)S(1)} %get-tuple-element.38), channel_id=1, source_target_pairs={{0,24},{4,28},{8,16},{12,20},{16,8},{20,12},{24,0},{28,4},{1,25},{... | collective-permute-start | bytes 251912 | tf_op jit(solution)/shard_map/ppermute | solution.py:36
  45.3 4.8 %collective-permute-start.10 = (bf16[328,128]{1,0:T(8,128)(2,1)S(1)}, bf16[328,128]{1,0:T(8,128)(2,1)S(1)}, u32[]{:S(2)}, u32[]{:S(2)}) collective-permute-start(bf16[328,128]{1,0:T(8,128)(2,1)S(1)} %get-tuple-element.39), channel_id=1, source_target_pairs={{0,8},{4,20},{8,0},{12,28},{16,24},{20,4},{24,16},{28,12},{1,9},{5... | collective-permute-start | bytes 251912 | tf_op jit(solution)/shard_map/ppermute | solution.py:36
  46.8 4.5 %collective-permute-start.11 = (bf16[328,128]{1,0:T(8,128)(2,1)S(1)}, bf16[328,128]{1,0:T(8,128)(2,1)S(1)}, u32[]{:S(2)}, u32[]{:S(2)}) collective-permute-start(bf16[328,128]{1,0:T(8,128)(2,1)S(1)} %get-tuple-element.40), channel_id=1, source_target_pairs={{0,16},{4,12},{8,24},{12,4},{16,0},{20,28},{24,8},{28,20},{1,17},{... | collective-permute-start | bytes 251912 | tf_op jit(solution)/shard_map/ppermute | solution.py:36
  51.6 1.5 %collective-permute-start.22 = (bf16[176,640]{1,0:T(8,128)(2,1)S(1)}, bf16[176,640]{1,0:T(8,128)(2,1)S(1)}, u32[]{:S(2)}, u32[]{:S(2)}) collective-permute-start(bf16[176,640]{1,0:T(8,128)(2,1)S(1)} %get-tuple-element.55), channel_id=1, source_target_pairs={{0,4},{4,0},{8,12},{12,8},{16,20},{20,16},{24,28},{28,24},{1,5},{5... | collective-permute-start | bytes 675848 | tf_op jit(solution)/shard_map/ppermute | solution.py:36
